TPU v7x, 32 devices: a whole 2x2x4 slice. The times are simulated.
32 devices in a mesh: section: 2 (over y), expert: 16 (over z, x, core).
Axes of the slice: x: 2, y: 2, z: 4, core: 2. Of those that a mesh axis runs over, the one named last changes fastest.
Arguments:
- reference_act: bfloat16 [2, 1024, 2048], P('section', 'expert'), may hold values from -6 to 6
- codes: int32 [2, 1024, 2048], P('section', 'expert'), may hold values from -127 to 127
- scale_index: int32 [2, 1024], P('section', 'expert'), may hold values from 0 to 15
- scale_table: float32 [16], replicated, may hold values from 0.002 to 0.02
- norm_gain: float32 [2, 2048], P('section'), may hold values from 0.25 to 1.75
- routes_fwd: int32 [2, 1024, 8], P('section', 'expert'), may hold values from 0 to 15, all different within a row; in each aligned block of 64 rows (0 to 63, 64 to 127, ..., all dimensions but the last counted through in order) at most 48 rows name the same one
- probs_fwd: float32 [2, 1024, 8], P('section', 'expert'), may hold values from 0.03 to 0.4
- gate_weight: bfloat16 [2, 16, 2048, 768], P('section', 'expert'), may hold values from -0.125 to 0.125
- up_weight: bfloat16 [2, 16, 2048, 768], P('section', 'expert'), may hold values from -0.125 to 0.125
- down_weight: bfloat16 [2, 16, 768, 2048], P('section', 'expert'), may hold values from -0.21875 to 0.21875
- saved_input: bfloat16 [2, 1024, 2048], P('section', 'expert'), may hold values from -6 to 6
- routes_bwd: int32 [2, 1024, 8], P('section', 'expert'), may hold values from 0 to 15, all different within a row; in each aligned block of 64 rows (0 to 63, 64 to 127, ..., all dimensions but the last counted through in order) at most 48 rows name the same one
- probs_bwd: float32 [2, 1024, 8], P('section', 'expert'), may hold values from 0.03 to 0.4
- saved_preact: bfloat16 [2, 16, 768, 1536], P('section', 'expert'), may hold values from -8 to 8
- cotangent: bfloat16 [2, 1024, 2048], P('section', 'expert'), may hold values from -6 to 6
Outputs:
- mixed: bfloat16 [2, 1024, 2048], P('section', 'expert')
- grad_input: bfloat16 [2, 1024, 2048], P('section', 'expert')
Inputs may be any that keep to these rules, and one draw needn't show every extreme that they name: `routes_fwd`: the 8 ids of a token differ; among the tokens of one device no expert is named more than 48 times, a bound that some block reaches. `routes_bwd`: the 8 ids of a token differ; among the tokens of one device no expert is named more than 48 times, a bound that some block reaches.
All inputs are finite; a program needn't handle non-finite values.
Results may differ from a plain program's by a relative error of at most 0.0051.
Values may be sent and summed in bfloat16 or wider, within the bound.
No kernel may reach another device: no remote copies, remote signals or barrier semaphores. Data moves between devices by JAX's collectives and lax.ppermute only.
A program may use at most 128 MiB of HBM per device.

v0:
```python
import jax
import jax.numpy as jnp
import numpy as np
from jax import lax
from jax.experimental import pallas as pl
from jax.experimental.pallas import tpu as pltpu
from jax.sharding import PartitionSpec as P

EPSILON = 1e-06
NORM_FLOPS = 4_000_000_000
PREPARE_FLOPS = 8_000_000_000


def from_behind(block, axis, distance):
    devices = range(lax.axis_size(axis))
    route = [(i - distance, i) for i in devices if i - distance in devices]
    return lax.ppermute(block, axis, route)


def shifted(x, axis, by):
    size = lax.axis_size(axis)
    return lax.ppermute(x, axis, [(i, (i + by) % size) for i in range(size)])


def inverse_rms(values):
    return lax.rsqrt(jnp.mean(values * values, axis=-1, keepdims=True) + EPSILON)


class Grid:
    def __init__(self, size):
        assert size >= 8 and size & (size - 1) == 0
        self.size = size
        self.outer = size // 4
        self.groups = [(k, k + 1) for k in range(0, self.outer, 2)]

    def swap(self, x, bits):
        return lax.ppermute(x, "expert", [(i, i ^ bits) for i in range(self.size)])

    def numbers(self, group):
        flips = [0] + [4 * k + f for f in (0, 2, 1, 3) for k in group]
        return lax.axis_index("expert") ^ np.array(flips, np.int32)

    def gather(self, x):
        near = {0: x}
        for k in range(1, self.outer):
            low = k & -k
            near[k] = self.swap(near[k - low], 4 * low)
        pieces = []
        for group in self.groups:
            own = [near[k] for k in group]
            other, own_beside, other_beside = [], [], []
            for k in group:
                other.append(self.swap(near[k], 2))
                own_beside.append(self.swap(near[k], 1))
                other_beside.append(self.swap(other[-1], 1))
            pieces.append(own + other + own_beside + other_beside)
        return pieces

    def scatter_sum(self, partials):
        f32, bf16 = jnp.float32, jnp.bfloat16
        total = {}
        for group, piece in zip(self.groups, partials):
            own, other, own_beside, other_beside = piece
            other_beside = self.swap(other_beside, 1)
            own_beside = self.swap(own_beside, 1)
            sent = (other.astype(f32) + other_beside.astype(f32)).astype(bf16)
            crossed = self.swap(sent, 2)
            near = own.astype(f32) + own_beside.astype(f32) + crossed.astype(f32)
            block = own.shape[0] // len(group)
            for i, k in enumerate(group):
                total[k] = near[i * block : (i + 1) * block]
        for k in sorted(total, key=lambda k: (-bin(k).count("1"), -k)):
            low = k & -k
            if k:
                part = self.swap(total[k].astype(bf16), 4 * low)
                total[k - low] = total[k - low] + part.astype(f32)
        return total[0]


NT = (((1,), (1,)), ((), ()))
VMEM = pl.BlockSpec(memory_space=pltpu.VMEM)
SMEM = pl.BlockSpec(memory_space=pltpu.SMEM)
ANY = pl.BlockSpec(memory_space=pl.ANY)


def own_weight(table, me, first, experts):
    lane = lax.broadcasted_iota(jnp.int32, table.shape, 1)
    high = first * experts + me
    here = (lane == high) | (lane == high + experts)
    return jnp.sum(jnp.where(here, table, 0.0), axis=1, keepdims=True)


def put_rows(out, outs):
    start = 0
    for ref in outs:
        ref[...] = out[start : start + ref.shape[0]]
        start += ref.shape[0]


def forward_kernel(experts, pieces, ids, *refs):
    f32, bf16 = jnp.float32, jnp.bfloat16
    blocks, tables, refs = refs[:pieces], refs[pieces : 2 * pieces], refs[2 * pieces :]
    wg, wu, wd, oa, ob, oc, od = refs
    table = jnp.concatenate([t[...] for t in tables], axis=0).astype(f32)
    weight = own_weight(table, ids[0], 0, experts)
    rows = jnp.concatenate([r[...] for r in blocks], axis=0)
    gate = jnp.dot(rows, wg[...], preferred_element_type=f32)
    up = jnp.dot(rows, wu[...], preferred_element_type=f32)
    hidden = (gate * jax.nn.sigmoid(gate) * up).astype(bf16)
    out = jnp.dot(hidden, wd[...], preferred_element_type=f32)
    put_rows((out * weight).astype(bf16), (oa, ob, oc, od))


def prepare_kernel(ids, stored, slopes):
    hidden_units = stored.shape[2] // 2

    def block(i, carry):
        kept = stored[i].astype(jnp.float32)
        gate, up = kept[:, :hidden_units], kept[:, hidden_units:]
        sigma = jax.nn.sigmoid(gate)
        slope = up * sigma * (1.0 + gate * (1.0 - sigma))
        slopes[i] = jnp.concatenate([slope, gate * sigma], axis=1).astype(jnp.bfloat16)
        return carry

    lax.fori_loop(0, stored.shape[0], block, 0)


def prepare(ids, stored):
    return pl.pallas_call(
        prepare_kernel,
        out_shape=jax.ShapeDtypeStruct(stored.shape, stored.dtype),
        in_specs=[SMEM, VMEM],
        out_specs=VMEM,
        compiler_params=pltpu.CompilerParams(vmem_limit_bytes=12 << 20),
        cost_estimate=pl.CostEstimate(
            flops=PREPARE_FLOPS, bytes_accessed=4 * stored.size, transcendentals=stored.size
        ),
        name="prepare",
    )(ids, stored)


def backward_kernel(experts, pieces, ids, *refs):
    f32, bf16 = jnp.float32, jnp.bfloat16
    carried, refs = refs[:pieces], refs[pieces:]
    stored, wg, wu, wd, oa, ob, oc, od = refs
    capacity = stored.shape[1]
    tokens = carried[0].shape[0]
    hidden_units = wg.shape[1]
    width = oa.shape[1]
    table = jnp.concatenate([r[:, width:] for r in carried], axis=0).astype(f32)
    weight = own_weight(table, ids[0], 2, experts)
    rows = jnp.concatenate([r[:, :width] for r in carried], axis=0)

    below = lax.broadcasted_iota(jnp.int32, (tokens, tokens), 0)
    below = (below > lax.broadcasted_iota(jnp.int32, (tokens, tokens), 1)).astype(bf16)
    column = lax.broadcasted_iota(jnp.int32, (tokens, capacity), 1).astype(f32)
    grad_hidden = lax.dot_general(rows, wd[...], NT, preferred_element_type=f32)
    grad_gates, grad_ups = [], []
    for i in range(pieces):
        part = slice(i * tokens, (i + 1) * tokens)
        named = weight[part] > 0
        ones = jnp.broadcast_to(jnp.where(named, 1.0, 0.0), (tokens, 128)).astype(bf16)
        earlier = jnp.dot(below, ones, preferred_element_type=f32)[:, :1]
        slot = jnp.where(named, earlier, -1.0)
        pick = (column == slot).astype(f32).astype(bf16)
        placed = jnp.dot(pick, stored[ids[1 + i]], preferred_element_type=f32)
        hidden = grad_hidden[part]
        grad_gates.append((hidden * placed[:, :hidden_units]).astype(bf16))
        grad_ups.append((hidden * placed[:, hidden_units:]).astype(bf16))
    grad_gate = jnp.concatenate(grad_gates, axis=0)
    grad_up = jnp.concatenate(grad_ups, axis=0)
    out = lax.dot_general(grad_gate, wg[...], NT, preferred_element_type=f32)
    out = out + lax.dot_general(grad_up, wu[...], NT, preferred_element_type=f32)
    put_rows((out * weight).astype(bf16), (oa, ob, oc, od))


def expert_forward(ids, rows, carried, weights, experts):
    width = rows[0].shape[1]
    hidden_units = weights[0].shape[1]
    side = carried[0].shape[1] - width
    total = sum(r.shape[0] for r in rows)
    tables = [
        pl.BlockSpec((c.shape[0], side), lambda i, at=width // side: (0, at)) for c in carried
    ]
    whole = [pl.BlockSpec(r.shape, lambda i: (0, 0)) for r in rows]
    return pl.pallas_call(
        lambda *refs: forward_kernel(experts, len(rows), *refs),
        grid=(1,),
        out_shape=[jax.ShapeDtypeStruct((total // 4, width), jnp.bfloat16)] * 4,
        in_specs=[SMEM] + whole + tables + [pl.BlockSpec(w.shape, lambda i: (0, 0)) for w in weights],
        out_specs=[pl.BlockSpec((total // 4, width), lambda i: (0, 0))] * 4,
        compiler_params=pltpu.CompilerParams(vmem_limit_bytes=28 << 20),
        cost_estimate=pl.CostEstimate(
            flops=6 * total * width * hidden_units, bytes_accessed=10 << 20, transcendentals=0
        ),
        name="expert_forward",
    )(ids, *rows, *carried, *weights)


def expert_backward(ids, carried, stored, weights, experts, width):
    hidden_units = weights[0].shape[1]
    total = sum(r.shape[0] for r in carried)
    blocks = len(carried)
    return pl.pallas_call(
        lambda *refs: backward_kernel(experts, blocks, *refs),
        out_shape=[jax.ShapeDtypeStruct((total // 4, width), jnp.bfloat16)] * 4,
        in_specs=[SMEM] + [VMEM] * (blocks + 4),
        out_specs=[VMEM] * 4,
        compiler_params=pltpu.CompilerParams(vmem_limit_bytes=28 << 20),
        cost_estimate=pl.CostEstimate(
            flops=6 * total * width * hidden_units, bytes_accessed=12 << 20, transcendentals=0
        ),
        name="expert_backward",
    )(ids, *carried, stored, *weights)


def norm_kernel(kept, received, gain, out):
    values = kept[...].astype(jnp.float32) + received[...].astype(jnp.float32)
    out[...] = (values * inverse_rms(values) * gain[...]).astype(jnp.bfloat16)


def normed_rows(kept, received, gain):
    return pl.pallas_call(
        norm_kernel,
        out_shape=jax.ShapeDtypeStruct(kept.shape, jnp.bfloat16),
        in_specs=[VMEM] * 3,
        out_specs=VMEM,
        compiler_params=pltpu.CompilerParams(vmem_limit_bytes=4 << 20),
        cost_estimate=pl.CostEstimate(flops=NORM_FLOPS, bytes_accessed=6 * kept.size, transcendentals=0),
        name="normed_rows",
    )(kept, received, gain)


def gradient_kernel(grad_normed, saved, grad_out, gain, out):
    saved_now = saved[...].astype(jnp.float32)
    scale = inverse_rms(saved_now)
    weighted = grad_normed[...] * gain[...]
    projection = jnp.mean(weighted * saved_now, axis=-1, keepdims=True)
    grad = grad_out[...].astype(jnp.float32) + scale * weighted
    out[...] = (grad - saved_now * scale * scale * scale * projection).astype(jnp.bfloat16)


def gradient_rows(grad_normed, saved, grad_out, gain):
    return pl.pallas_call(
        gradient_kernel,
        out_shape=jax.ShapeDtypeStruct(saved.shape, jnp.bfloat16),
        in_specs=[VMEM] * 4,
        out_specs=VMEM,
        compiler_params=pltpu.CompilerParams(vmem_limit_bytes=8 << 20),
        cost_estimate=pl.CostEstimate(
            flops=16 * saved.size, bytes_accessed=10 * saved.size, transcendentals=0
        ),
        name="gradient_rows",
    )(grad_normed, saved, grad_out, gain)


def dense_weights(routes, probs, experts):
    ids = jnp.arange(experts, dtype=jnp.int32)
    hit = routes[:, :, None] == ids[None, None, :]
    return jnp.sum(jnp.where(hit, probs[:, :, None], 0.0), axis=1)


def in_two(values):
    high = values.astype(jnp.bfloat16)
    low = (values - high.astype(jnp.float32)).astype(jnp.bfloat16)
    return [high, low]


def on_device(
    reference_act,
    codes,
    scale_index,
    scale_table,
    norm_gain,
    routes_fwd,
    probs_fwd,
    gate_weight,
    up_weight,
    down_weight,
    saved_input,
    routes_bwd,
    probs_bwd,
    saved_preact,
    cotangent,
):
    f32, bf16 = jnp.float32, jnp.bfloat16
    experts = lax.axis_size("expert")
    grid = Grid(experts)
    model_width = reference_act.shape[2]
    levels = scale_table.shape[0]
    weights = (gate_weight[0, 0], up_weight[0, 0], down_weight[0, 0])
    stored = saved_preact[0, 0].reshape(experts, -1, saved_preact.shape[3])

    numbers = [grid.numbers(group) for group in grid.groups]
    stored = prepare(jnp.concatenate(numbers), stored)
    grad_out = shifted(cotangent[0], "section", -1)
    picker = (scale_index[0][:, None] == jnp.arange(levels, dtype=jnp.int32)[None, :]).astype(f32)
    row_scale = jnp.sum(picker * scale_table[None, :], axis=1)
    delta_rows = (codes[0].astype(f32) * row_scale[:, None]).astype(bf16)
    received = from_behind(delta_rows, "section", 1)

    table = in_two(dense_weights(routes_fwd[0], probs_fwd[0], experts))
    table += in_two(dense_weights(routes_bwd[0], probs_bwd[0], experts))
    table = jnp.concatenate(table, axis=1)
    table = jnp.pad(table, ((0, 0), (0, -table.shape[1] % 128)))
    carried = grid.gather(jnp.concatenate([grad_out, table], axis=1))

    inputs_now = reference_act[0].astype(f32) + received.astype(f32)
    normed = normed_rows(reference_act[0], received, norm_gain)
    rows = grid.gather(normed)

    slot_grads = []
    for ids, piece in zip(numbers, carried):
        slot_grads.append(
            expert_backward(ids, piece, stored, weights, experts, model_width)
        )
    grad_normed = grid.scatter_sum(slot_grads)
    produced = []
    for ids, piece, side in zip(numbers, rows, carried):
        produced.append(expert_forward(ids, piece, side, weights, experts))
    mixed = inputs_now + grid.scatter_sum(produced)

    grad_now = gradient_rows(grad_normed, saved_input[0], grad_out, norm_gain)
    return (mixed.astype(bf16)[None], grad_now[None])


def solution(mesh):
    step = jax.shard_map(
        on_device,
        mesh=mesh,
        in_specs=(
            P("section", "expert", None),
            P("section", "expert", None),
            P("section", "expert"),
            P(),
            P("section", None),
            P("section", "expert", None),
            P("section", "expert", None),
            P("section", "expert", None, None),
            P("section", "expert", None, None),
            P("section", "expert", None, None),
            P("section", "expert", None),
            P("section", "expert", None),
            P("section", "expert", None),
            P("section", "expert", None, None),
            P("section", "expert", None),
        ),
        out_specs=(P("section", "expert", None), P("section", "expert", None)),
        check_vma=False,
    )
    if Grid(mesh.shape["expert"]).outer > 4:
        return step
    return step
```

profile of v0, /device:TPU:0, one launch (start us, length us, event | category | flops | bytes accessed | tf_op | source)
XLA Modules:
  0.0 183.9 jit_solution(3065967503397452490)
XLA Ops:
  0.6 3.1 %collective-permute-start.8 = (bf16[64,2048]{1,0:T(8,128)(2,1)}, bf16[64,2048]{1,0:T(8,128)(2,1)S(1)}, u32[]{:S(2)}, u32[]{:S(2)}) collective-permute-start(bf16[64,2048]{1,0:T(8,128)(2,1)} %bitcast.40), channel_id=1, source_target_pairs={{0,16},{16,0},{1,17},{17,1},{2,18},{18,2},{3,19},{19,3},{4,20},{20... | collective-permute-start | bytes 786440 | tf_op jit(solution)/shard_map/ppermute | solution.py:22
  3.7 0.8 select_reduce_fusion.2
  4.4 1.1 fusion.6
  5.6 1.9 %collective-permute-start = (bf16[64,2048]{1,0:T(8,128)(2,1)S(1)}, bf16[64,2048]{1,0:T(8,128)(2,1)S(1)}, u32[]{:S(2)}, u32[]{:S(2)}) collective-permute-start(bf16[64,2048]{1,0:T(8,128)(2,1)S(1)} %fusion.6), channel_id=1, source_target_pairs={{0,16},{1,17},{2,18},{3,19},{4,20},{5,21},{6,22},{7,23},{8,24},{9,... | collective-permute-start | bytes 786440 | tf_op jit(solution)/shard_map/ppermute | solution.py:17
  7.5 0.7 select_reduce_fusion.1
  8.4 0.7 select_reduce_fusion
  9.5 5.6 %collective-permute-done.received = bf16[64,2048]{1,0:T(8,128)(2,1)S(1)} collective-permute-done((bf16[64,2048]{1,0:T(8,128)(2,1)S(1)}, bf16[64,2048]{1,0:T(8,128)(2,1)S(1)}, u32[]{:S(2)}, u32[]{:S(2)}) %collective-permute-start) | collective-permute-done | bytes 262176 | tf_op jit(solution)/shard_map/ppermute | solution.py:17
  15.1 0.9 copy-done.1
  16.7 0.9 normed_rows.1.refs_1_
  17.6 2.6 %collective-permute-start.19 = (bf16[64,2048]{1,0:T(8,128)(2,1)}, bf16[64,2048]{1,0:T(8,128)(2,1)}, u32[]{:S(2)}, u32[]{:S(2)}) collective-permute-start(bf16[64,2048]{1,0:T(8,128)(2,1)} %normed_rows.1.refs_1_), channel_id=1, source_target_pairs={{0,8},{1,9},{2,10},{3,11},{4,12},{5,13},{6,14},{7,15},{8,0},{9,1},... | collective-permute-start | bytes 786440 | tf_op jit(solution)/shard_map/ppermute | solution.py:37
  20.6 1.6 collective-permute-start.9
  22.7 1.5 collective-permute-start.2
  24.2 14.7 %collective-permute-done.19.refs_1_ = bf16[64,2048]{1,0:T(8,128)(2,1)} collective-permute-done((bf16[64,2048]{1,0:T(8,128)(2,1)}, bf16[64,2048]{1,0:T(8,128)(2,1)}, u32[]{:S(2)}, u32[]{:S(2)}) %collective-permute-start.19) | collective-permute-done | bytes 262176 | tf_op jit(solution)/shard_map/ppermute | solution.py:37
  38.8 5.0 %collective-permute-done.1.refs_2_ = bf16[64,2048]{1,0:T(8,128)(2,1)} collective-permute-done((bf16[64,2048]{1,0:T(8,128)(2,1)}, bf16[64,2048]{1,0:T(8,128)(2,1)}, u32[]{:S(2)}, u32[]{:S(2)}) %collective-permute-start.1) | collective-permute-done | bytes 262176 | tf_op jit(solution)/shard_map/ppermute | solution.py:37
  43.8 1.5 collective-permute-start.10
  45.3 1.5 collective-permute-start.20
  47.4 1.5 collective-permute-start.11
  49.0 1.9 %collective-permute-done.10.refs_11_.refs_3_ = bf16[64,2176]{1,0:T(8,128)(2,1)S(1)} collective-permute-done((bf16[64,2176]{1,0:T(8,128)(2,1)S(1)}, bf16[64,2176]{1,0:T(8,128)(2,1)S(1)}, u32[]{:S(2)}, u32[]{:S(2)}) %collective-permute-start.10) | collective-permute-done | bytes 278560 | tf_op jit(solution)/shard_map/ppermute | solution.py:37
  50.9 2.5 %collective-permute-start.3 = (bf16[64,2048]{1,0:T(8,128)(2,1)}, bf16[64,2048]{1,0:T(8,128)(2,1)S(1)}, u32[]{:S(2)}, u32[]{:S(2)}) collective-permute-start(bf16[64,2048]{1,0:T(8,128)(2,1)} %collective-permute-done.1.refs_2_), channel_id=1, source_target_pairs={{0,2},{1,3},{2,0},{3,1},{4,6},{5,7},{6,4},{7,5},{8,10},{9,11},{10,... | collective-permute-start | bytes 786440 | tf_op jit(solution)/shard_map/ppermute | solution.py:37
  53.4 0.9 collective-permute-done.20.refs_2_
  54.3 1.9 %collective-permute-start.28 = (bf16[64,2176]{1,0:T(8,128)(2,1)S(1)}, bf16[64,2176]{1,0:T(8,128)(2,1)S(1)}, u32[]{:S(2)}, u32[]{:S(2)}) collective-permute-start(bf16[64,2176]{1,0:T(8,128)(2,1)S(1)} %collective-permute-done.27.refs_9_.refs_1_), channel_id=1, source_target_pairs={{0,4},{1,5},{2,6},{3,7},{4,0},{5,1},{6,2},{7,3},{8,12},{9,13},{10,... | collective-permute-start | bytes 835592 | tf_op jit(solution)/shard_map/ppermute | solution.py:37
  56.6 6.0 %collective-permute-done.11.refs_12_.refs_4_ = bf16[64,2176]{1,0:T(8,128)(2,1)S(1)} collective-permute-done((bf16[64,2176]{1,0:T(8,128)(2,1)}, bf16[64,2176]{1,0:T(8,128)(2,1)S(1)}, u32[]{:S(2)}, u32[]{:S(2)}) %collective-permute-start.11) | collective-permute-done | bytes 278560 | tf_op jit(solution)/shard_map/ppermute | solution.py:37
  62.6 1.5 prepare.1.refs_9_
  64.1 3.5 %collective-permute-done.3.refs_4_ = bf16[64,2048]{1,0:T(8,128)(2,1)S(1)} collective-permute-done((bf16[64,2048]{1,0:T(8,128)(2,1)}, bf16[64,2048]{1,0:T(8,128)(2,1)S(1)}, u32[]{:S(2)}, u32[]{:S(2)}) %collective-permute-start.3) | collective-permute-done | bytes 262176 | tf_op jit(solution)/shard_map/ppermute | solution.py:37
  68.1 1.5 collective-permute-start.29
  70.2 8.0 %expert_backward.2 = (bf16[128,2048]{1,0:T(8,128)(2,1)S(1)}, bf16[128,2048]{1,0:T(8,128)(2,1)S(1)}, bf16[128,2048]{1,0:T(8,128)(2,1)S(1)}, bf16[128,2048]{1,0:T(8,128)(2,1)S(1)}) custom-call(s32[9]{0:T(128)S(1)} %broadcast_xor_fusion.1.refs_0_, bf16[64,2176]{1,0:T(8,128)(2,1)S(1)} %pad_maximum_fusion.refs_9_.refs_1_, ...), custom_call_target="tpu_custom_call" | custom-call | flops 4831838208 | bytes 12582912 | tf_op jit(solution)/shard_map/expert_backward/pallas_call | solution.py:204
  78.5 1.5 collective-permute-start.22
  80.5 3.1 %collective-permute-done.30.refs_12_.refs_4_ = bf16[64,2176]{1,0:T(8,128)(2,1)S(1)} collective-permute-done((bf16[64,2176]{1,0:T(8,128)(2,1)S(1)}, bf16[64,2176]{1,0:T(8,128)(2,1)S(1)}, u32[]{:S(2)}, u32[]{:S(2)}) %collective-permute-start.30) | collective-permute-done | bytes 278560 | tf_op jit(solution)/shard_map/ppermute | solution.py:37
  83.6 6.3 %expert_forward.2 = (bf16[128,2048]{1,0:T(8,128)(2,1)S(1)}, bf16[128,2048]{1,0:T(8,128)(2,1)S(1)}, bf16[128,2048]{1,0:T(8,128)(2,1)S(1)}, bf16[128,2048]{1,0:T(8,128)(2,1)S(1)}) custom-call(s32[9]{0:T(128)S(1)} %broadcast_xor_fusion.1.refs_0_, bf16[64,2048]{1,0:T(8,128)(2,1)} %normed_rows.1.refs_1_, bf16[64,2048]{1,0:T(8,128)(2,1)} %collective-permute-done.1.refs_2_, ...), custom_call_target="tpu_custom_call" | custom-call | flops 4831838208 | bytes 10485760 | tf_op jit(solution)/shard_map/expert_forward/pallas_call | solution.py:186
  91.5 7.8 %expert_backward.3 = (bf16[128,2048]{1,0:T(8,128)(2,1)S(1)}, bf16[128,2048]{1,0:T(8,128)(2,1)S(1)}, bf16[128,2048]{1,0:T(8,128)(2,1)S(1)}, bf16[128,2048]{1,0:T(8,128)(2,1)S(1)}) custom-call(s32[9]{0:T(128)S(1)} %broadcast_xor_fusion.refs_0_, bf16[64,2176]{1,0:T(8,128)(2,1)S(1)} %collective-permute-done.27.refs_9_.refs_1_, ...), custom_call_target="tpu_custom_call" | custom-call | flops 4831838208 | bytes 12582912 | tf_op jit(solution)/shard_map/expert_backward/pallas_call | solution.py:204
  100.4 6.0 %expert_forward.3 = (bf16[128,2048]{1,0:T(8,128)(2,1)S(1)}, bf16[128,2048]{1,0:T(8,128)(2,1)S(1)}, bf16[128,2048]{1,0:T(8,128)(2,1)S(1)}, bf16[128,2048]{1,0:T(8,128)(2,1)S(1)}) custom-call(s32[9]{0:T(128)S(1)} %broadcast_xor_fusion.refs_0_, bf16[64,2048]{1,0:T(8,128)(2,1)} %collective-permute-done.19.refs_1_, ...), custom_call_target="tpu_custom_call" | custom-call | flops 4831838208 | bytes 10485760 | tf_op jit(solution)/shard_map/expert_forward/pallas_call | solution.py:186
  107.4 1.6 collective-permute-start.43
  109.2 1.5 collective-permute-start.18
  110.9 11.3 %collective-permute-done.43 = bf16[128,2048]{1,0:T(8,128)(2,1)S(1)} collective-permute-done((bf16[128,2048]{1,0:T(8,128)(2,1)S(1)}, bf16[128,2048]{1,0:T(8,128)(2,1)S(1)}, u32[]{:S(2)}, u32[]{:S(2)}) %collective-permute-start.43) | collective-permute-done | bytes 524320 | tf_op jit(solution)/shard_map/ppermute | solution.py:37
  122.3 1.5 collective-permute-start.46
  124.6 8.9 %collective-permute-done.18 = bf16[128,2048]{1,0:T(8,128)(2,1)S(1)} collective-permute-done((bf16[128,2048]{1,0:T(8,128)(2,1)S(1)}, bf16[128,2048]{1,0:T(8,128)(2,1)S(1)}, u32[]{:S(2)}, u32[]{:S(2)}) %collective-permute-start.18) | collective-permute-done | bytes 524320 | tf_op jit(solution)/shard_map/ppermute | solution.py:37
  133.5 1.7 collective-permute-start.49
  135.9 8.9 %collective-permute-done.46 = bf16[128,2048]{1,0:T(8,128)(2,1)S(1)} collective-permute-done((bf16[128,2048]{1,0:T(8,128)(2,1)S(1)}, bf16[128,2048]{1,0:T(8,128)(2,1)S(1)}, u32[]{:S(2)}, u32[]{:S(2)}) %collective-permute-start.46) | collective-permute-done | bytes 524320 | tf_op jit(solution)/shard_map/ppermute | solution.py:37
  145.0 1.7 collective-permute-start.47
  146.7 8.4 %collective-permute-done.37 = bf16[128,2048]{1,0:T(8,128)(2,1)S(1)} collective-permute-done((bf16[128,2048]{1,0:T(8,128)(2,1)S(1)}, bf16[128,2048]{1,0:T(8,128)(2,1)S(1)}, u32[]{:S(2)}, u32[]{:S(2)}) %collective-permute-start.37) | collective-permute-done | bytes 524320 | tf_op jit(solution)/shard_map/ppermute | solution.py:37
  155.4 1.7 collective-permute-start.38
  157.1 3.6 %collective-permute-start.48 = (bf16[64,2048]{1,0:T(8,128)(2,1)S(1)}, bf16[64,2048]{1,0:T(8,128)(2,1)S(1)}, u32[]{:S(2)}, u32[]{:S(2)}) collective-permute-start(bf16[64,2048]{1,0:T(8,128)(2,1)S(1)} %fusion), channel_id=1, source_target_pairs={{0,8},{1,9},{2,10},{3,11},{4,12},{5,13},{6,14},{7,15},{8,0},{9,1},... | collective-permute-start | bytes 786440 | tf_op jit(solution)/shard_map/ppermute | solution.py:37
  160.7 7.4 %collective-permute-done.38 = bf16[64,2048]{1,0:T(8,128)(2,1)S(1)} collective-permute-done((bf16[64,2048]{1,0:T(8,128)(2,1)S(1)}, bf16[64,2048]{1,0:T(8,128)(2,1)S(1)}, u32[]{:S(2)}, u32[]{:S(2)}) %collective-permute-start.38) | collective-permute-done | bytes 262176 | tf_op jit(solution)/shard_map/ppermute | solution.py:37
  168.2 1.0 collective-permute-start.39
  169.2 8.6 %collective-permute-done.48 = bf16[64,2048]{1,0:T(8,128)(2,1)S(1)} collective-permute-done((bf16[64,2048]{1,0:T(8,128)(2,1)S(1)}, bf16[64,2048]{1,0:T(8,128)(2,1)S(1)}, u32[]{:S(2)}, u32[]{:S(2)}) %collective-permute-start.48) | collective-permute-done | bytes 262176 | tf_op jit(solution)/shard_map/ppermute | solution.py:37
  177.9 1.1 gradient_rows.1
  179.0 4.1 %collective-permute-done.39 = bf16[64,2048]{1,0:T(8,128)(2,1)S(1)} collective-permute-done((bf16[64,2048]{1,0:T(8,128)(2,1)S(1)}, bf16[64,2048]{1,0:T(8,128)(2,1)S(1)}, u32[]{:S(2)}, u32[]{:S(2)}) %collective-permute-start.39) | collective-permute-done | bytes 262176 | tf_op jit(solution)/shard_map/ppermute | solution.py:37
  183.0 0.9 fusion.7
  (113 shorter events, 11.2 us)
Async XLA Ops:
  0.6 19.6 %collective-permute-start.8 = (bf16[64,2048]{1,0:T(8,128)(2,1)}, bf16[64,2048]{1,0:T(8,128)(2,1)S(1)}, u32[]{:S(2)}, u32[]{:S(2)}) collective-permute-start(bf16[64,2048]{1,0:T(8,128)(2,1)} %bitcast.40), channel_id=1, source_target_pairs={{0,16},{16,0},{1,17},{17,1},{2,18},{18,2},{3,19},{19,3},{4,20},{20... | collective-permute-start | bytes 786440 | tf_op jit(solution)/shard_map/ppermute | solution.py:22
  5.6 9.5 %collective-permute-start = (bf16[64,2048]{1,0:T(8,128)(2,1)S(1)}, bf16[64,2048]{1,0:T(8,128)(2,1)S(1)}, u32[]{:S(2)}, u32[]{:S(2)}) collective-permute-start(bf16[64,2048]{1,0:T(8,128)(2,1)S(1)} %fusion.6), channel_id=1, source_target_pairs={{0,16},{1,17},{2,18},{3,19},{4,20},{5,21},{6,22},{7,23},{8,24},{9,... | collective-permute-start | bytes 786440 | tf_op jit(solution)/shard_map/ppermute | solution.py:17
  17.6 21.2 %collective-permute-start.19 = (bf16[64,2048]{1,0:T(8,128)(2,1)}, bf16[64,2048]{1,0:T(8,128)(2,1)}, u32[]{:S(2)}, u32[]{:S(2)}) collective-permute-start(bf16[64,2048]{1,0:T(8,128)(2,1)} %normed_rows.1.refs_1_), channel_id=1, source_target_pairs={{0,8},{1,9},{2,10},{3,11},{4,12},{5,13},{6,14},{7,15},{8,0},{9,1},... | collective-permute-start | bytes 786440 | tf_op jit(solution)/shard_map/ppermute | solution.py:37
  20.2 26.6 %collective-permute-start.27 = (bf16[64,2176]{1,0:T(8,128)(2,1)S(1)}, bf16[64,2176]{1,0:T(8,128)(2,1)S(1)}, u32[]{:S(2)}, u32[]{:S(2)}) collective-permute-start(bf16[64,2176]{1,0:T(8,128)(2,1)S(1)} %pad_maximum_fusion.refs_9_.refs_1_), channel_id=1, source_target_pairs={{0,8},{1,9},{2,10},{3,11},{4,12},{5,13},{6,14},{7,15},{8,0},{9,1},... | collective-permute-start | bytes 835592 | tf_op jit(solution)/shard_map/ppermute | solution.py:37
  20.6 26.8 %collective-permute-start.9 = (bf16[64,2176]{1,0:T(8,128)(2,1)S(1)}, bf16[64,2176]{1,0:T(8,128)(2,1)}, u32[]{:S(2)}, u32[]{:S(2)}) collective-permute-start(bf16[64,2176]{1,0:T(8,128)(2,1)S(1)} %pad_maximum_fusion.refs_9_.refs_1_), channel_id=1, source_target_pairs={{0,4},{1,5},{2,6},{3,7},{4,0},{5,1},{6,2},{7,3},{8,12},{9,13},{10,... | collective-permute-start | bytes 835592 | tf_op jit(solution)/shard_map/ppermute | solution.py:37
  22.2 21.6 %collective-permute-start.1 = (bf16[64,2048]{1,0:T(8,128)(2,1)}, bf16[64,2048]{1,0:T(8,128)(2,1)}, u32[]{:S(2)}, u32[]{:S(2)}) collective-permute-start(bf16[64,2048]{1,0:T(8,128)(2,1)} %normed_rows.1.refs_1_), channel_id=1, source_target_pairs={{0,4},{1,5},{2,6},{3,7},{4,0},{5,1},{6,2},{7,3},{8,12},{9,13},{10,... | collective-permute-start | bytes 786440 | tf_op jit(solution)/shard_map/ppermute | solution.py:37
  22.7 22.7 %collective-permute-start.2 = (bf16[64,2048]{1,0:T(8,128)(2,1)}, bf16[64,2048]{1,0:T(8,128)(2,1)}, u32[]{:S(2)}, u32[]{:S(2)}) collective-permute-start(bf16[64,2048]{1,0:T(8,128)(2,1)} %normed_rows.1.refs_1_), channel_id=1, source_target_pairs={{0,2},{1,3},{2,0},{3,1},{4,6},{5,7},{6,4},{7,5},{8,10},{9,11},{10,... | collective-permute-start | bytes 786440 | tf_op jit(solution)/shard_map/ppermute | solution.py:37
  43.8 7.1 %collective-permute-start.10 = (bf16[64,2176]{1,0:T(8,128)(2,1)S(1)}, bf16[64,2176]{1,0:T(8,128)(2,1)S(1)}, u32[]{:S(2)}, u32[]{:S(2)}) collective-permute-start(bf16[64,2176]{1,0:T(8,128)(2,1)S(1)} %pad_maximum_fusion.refs_9_.refs_1_), channel_id=1, source_target_pairs={{0,2},{1,3},{2,0},{3,1},{4,6},{5,7},{6,4},{7,5},{8,10},{9,11},{10,... | collective-permute-start | bytes 835592 | tf_op jit(solution)/shard_map/ppermute | solution.py:37
  45.3 8.0 %collective-permute-start.12 = (bf16[64,2176]{1,0:T(8,128)(2,1)S(1)}, bf16[64,2176]{1,0:T(8,128)(2,1)S(1)}, u32[]{:S(2)}, u32[]{:S(2)}) collective-permute-start(bf16[64,2176]{1,0:T(8,128)(2,1)S(1)} %pad_maximum_fusion.refs_9_.refs_1_), channel_id=1, source_target_pairs={{0,1},{1,0},{2,3},{3,2},{4,5},{5,4},{6,7},{7,6},{8,9},{9,8},{10,11... | collective-permute-start | bytes 835592 | tf_op jit(solution)/shard_map/ppermute | solution.py:37
  45.3 8.9 %collective-permute-start.20 = (bf16[64,2048]{1,0:T(8,128)(2,1)}, bf16[64,2048]{1,0:T(8,128)(2,1)S(1)}, u32[]{:S(2)}, u32[]{:S(2)}) collective-permute-start(bf16[64,2048]{1,0:T(8,128)(2,1)} %collective-permute-done.19.refs_1_), channel_id=1, source_target_pairs={{0,4},{1,5},{2,6},{3,7},{4,0},{5,1},{6,2},{7,3},{8,12},{9,13},{10,... | collective-permute-start | bytes 786440 | tf_op jit(solution)/shard_map/ppermute | solution.py:37
  46.9 9.7 %collective-permute-start.21 = (bf16[64,2048]{1,0:T(8,128)(2,1)}, bf16[64,2048]{1,0:T(8,128)(2,1)S(1)}, u32[]{:S(2)}, u32[]{:S(2)}) collective-permute-start(bf16[64,2048]{1,0:T(8,128)(2,1)} %collective-permute-done.19.refs_1_), channel_id=1, source_target_pairs={{0,2},{1,3},{2,0},{3,1},{4,6},{5,7},{6,4},{7,5},{8,10},{9,11},{10,... | collective-permute-start | bytes 786440 | tf_op jit(solution)/shard_map/ppermute | solution.py:37
  47.4 15.2 %collective-permute-start.11 = (bf16[64,2176]{1,0:T(8,128)(2,1)}, bf16[64,2176]{1,0:T(8,128)(2,1)S(1)}, u32[]{:S(2)}, u32[]{:S(2)}) collective-permute-start(bf16[64,2176]{1,0:T(8,128)(2,1)} %collective-permute-done.9.refs_10_.refs_2_), channel_id=1, source_target_pairs={{0,2},{1,3},{2,0},{3,1},{4,6},{5,7},{6,4},{7,5},{8,10},{9,11},{10,... | collective-permute-start | bytes 835592 | tf_op jit(solution)/shard_map/ppermute | solution.py:37
  50.9 16.7 %collective-permute-start.3 = (bf16[64,2048]{1,0:T(8,128)(2,1)}, bf16[64,2048]{1,0:T(8,128)(2,1)S(1)}, u32[]{:S(2)}, u32[]{:S(2)}) collective-permute-start(bf16[64,2048]{1,0:T(8,128)(2,1)} %collective-permute-done.1.refs_2_), channel_id=1, source_target_pairs={{0,2},{1,3},{2,0},{3,1},{4,6},{5,7},{6,4},{7,5},{8,10},{9,11},{10,... | collective-permute-start | bytes 786440 | tf_op jit(solution)/shard_map/ppermute | solution.py:37
  53.4 14.7 %collective-permute-start.13 = (bf16[64,2176]{1,0:T(8,128)(2,1)}, bf16[64,2176]{1,0:T(8,128)(2,1)S(1)}, u32[]{:S(2)}, u32[]{:S(2)}) collective-permute-start(bf16[64,2176]{1,0:T(8,128)(2,1)} %collective-permute-done.9.refs_10_.refs_2_), channel_id=1, source_target_pairs={{0,1},{1,0},{2,3},{3,2},{4,5},{5,4},{6,7},{7,6},{8,9},{9,8},{10,11... | collective-permute-start | bytes 835592 | tf_op jit(solution)/shard_map/ppermute | solution.py:37
  54.3 13.3 %collective-permute-start.28 = (bf16[64,2176]{1,0:T(8,128)(2,1)S(1)}, bf16[64,2176]{1,0:T(8,128)(2,1)S(1)}, u32[]{:S(2)}, u32[]{:S(2)}) collective-permute-start(bf16[64,2176]{1,0:T(8,128)(2,1)S(1)} %collective-permute-done.27.refs_9_.refs_1_), channel_id=1, source_target_pairs={{0,4},{1,5},{2,6},{3,7},{4,0},{5,1},{6,2},{7,3},{8,12},{9,13},{10,... | collective-permute-start | bytes 835592 | tf_op jit(solution)/shard_map/ppermute | solution.py:37
  56.6 13.0 %collective-permute-start.14 = (bf16[64,2176]{1,0:T(8,128)(2,1)S(1)}, bf16[64,2176]{1,0:T(8,128)(2,1)S(1)}, u32[]{:S(2)}, u32[]{:S(2)}) collective-permute-start(bf16[64,2176]{1,0:T(8,128)(2,1)S(1)} %collective-permute-done.10.refs_11_.refs_3_), channel_id=1, source_target_pairs={{0,1},{1,0},{2,3},{3,2},{4,5},{5,4},{6,7},{7,6},{8,9},{9,8},{10,11... | collective-permute-start | bytes 835592 | tf_op jit(solution)/shard_map/ppermute | solution.py:37
  62.6 7.0 %collective-permute-start.15 = (bf16[64,2176]{1,0:T(8,128)(2,1)S(1)}, bf16[64,2176]{1,0:T(8,128)(2,1)S(1)}, u32[]{:S(2)}, u32[]{:S(2)}) collective-permute-start(bf16[64,2176]{1,0:T(8,128)(2,1)S(1)} %collective-permute-done.11.refs_12_.refs_4_), channel_id=1, source_target_pairs={{0,1},{1,0},{2,3},{3,2},{4,5},{5,4},{6,7},{7,6},{8,9},{9,8},{10,11... | collective-permute-start | bytes 835592 | tf_op jit(solution)/shard_map/ppermute | solution.py:37
  67.6 10.7 %collective-permute-start.5 = (bf16[64,2048]{1,0:T(8,128)(2,1)}, bf16[64,2048]{1,0:T(8,128)(2,1)S(1)}, u32[]{:S(2)}, u32[]{:S(2)}) collective-permute-start(bf16[64,2048]{1,0:T(8,128)(2,1)} %collective-permute-done.1.refs_2_), channel_id=1, source_target_pairs={{0,1},{1,0},{2,3},{3,2},{4,5},{5,4},{6,7},{7,6},{8,9},{9,8},{10,11... | collective-permute-start | bytes 786440 | tf_op jit(solution)/shard_map/ppermute | solution.py:37
  67.6 10.9 %collective-permute-start.6 = (bf16[64,2048]{1,0:T(8,128)(2,1)}, bf16[64,2048]{1,0:T(8,128)(2,1)S(1)}, u32[]{:S(2)}, u32[]{:S(2)}) collective-permute-start(bf16[64,2048]{1,0:T(8,128)(2,1)} %collective-permute-done.2.refs_3_), channel_id=1, source_target_pairs={{0,1},{1,0},{2,3},{3,2},{4,5},{5,4},{6,7},{7,6},{8,9},{9,8},{10,11... | collective-permute-start | bytes 786440 | tf_op jit(solution)/shard_map/ppermute | solution.py:37
  68.1 11.9 %collective-permute-start.29 = (bf16[64,2176]{1,0:T(8,128)(2,1)S(1)}, bf16[64,2176]{1,0:T(8,128)(2,1)S(1)}, u32[]{:S(2)}, u32[]{:S(2)}) collective-permute-start(bf16[64,2176]{1,0:T(8,128)(2,1)S(1)} %collective-permute-done.27.refs_9_.refs_1_), channel_id=1, source_target_pairs={{0,2},{1,3},{2,0},{3,1},{4,6},{5,7},{6,4},{7,5},{8,10},{9,11},{10,... | collective-permute-start | bytes 835592 | tf_op jit(solution)/shard_map/ppermute | solution.py:37
  69.6 10.5 %collective-permute-start.7 = (bf16[64,2048]{1,0:T(8,128)(2,1)S(1)}, bf16[64,2048]{1,0:T(8,128)(2,1)S(1)}, u32[]{:S(2)}, u32[]{:S(2)}) collective-permute-start(bf16[64,2048]{1,0:T(8,128)(2,1)S(1)} %collective-permute-done.3.refs_4_), channel_id=1, source_target_pairs={{0,1},{1,0},{2,3},{3,2},{4,5},{5,4},{6,7},{7,6},{8,9},{9,8},{10,11... | collective-permute-start | bytes 786440 | tf_op jit(solution)/shard_map/ppermute | solution.py:37
  69.6 14.0 %collective-permute-start.30 = (bf16[64,2176]{1,0:T(8,128)(2,1)S(1)}, bf16[64,2176]{1,0:T(8,128)(2,1)S(1)}, u32[]{:S(2)}, u32[]{:S(2)}) collective-permute-start(bf16[64,2176]{1,0:T(8,128)(2,1)S(1)} %collective-permute-done.28.refs_10_.refs_2_), channel_id=1, source_target_pairs={{0,2},{1,3},{2,0},{3,1},{4,6},{5,7},{6,4},{7,5},{8,10},{9,11},{10,... | collective-permute-start | bytes 835592 | tf_op jit(solution)/shard_map/ppermute | solution.py:37
  78.3 11.7 %collective-permute-start.31 = (bf16[64,2176]{1,0:T(8,128)(2,1)S(1)}, bf16[64,2176]{1,0:T(8,128)(2,1)S(1)}, u32[]{:S(2)}, u32[]{:S(2)}) collective-permute-start(bf16[64,2176]{1,0:T(8,128)(2,1)S(1)} %collective-permute-done.27.refs_9_.refs_1_), channel_id=1, source_target_pairs={{0,1},{1,0},{2,3},{3,2},{4,5},{5,4},{6,7},{7,6},{8,9},{9,8},{10,11... | collective-permute-start | bytes 835592 | tf_op jit(solution)/shard_map/ppermute | solution.py:37
  78.5 12.0 %collective-permute-start.22 = (bf16[64,2048]{1,0:T(8,128)(2,1)S(1)}, bf16[64,2048]{1,0:T(8,128)(2,1)S(1)}, u32[]{:S(2)}, u32[]{:S(2)}) collective-permute-start(bf16[64,2048]{1,0:T(8,128)(2,1)S(1)} %collective-permute-done.20.refs_2_), channel_id=1, source_target_pairs={{0,2},{1,3},{2,0},{3,1},{4,6},{5,7},{6,4},{7,5},{8,10},{9,11},{10,... | collective-permute-start | bytes 786440 | tf_op jit(solution)/shard_map/ppermute | solution.py:37
  80.0 10.6 %collective-permute-start.32 = (bf16[64,2176]{1,0:T(8,128)(2,1)S(1)}, bf16[64,2176]{1,0:T(8,128)(2,1)S(1)}, u32[]{:S(2)}, u32[]{:S(2)}) collective-permute-start(bf16[64,2176]{1,0:T(8,128)(2,1)S(1)} %collective-permute-done.28.refs_10_.refs_2_), channel_id=1, source_target_pairs={{0,1},{1,0},{2,3},{3,2},{4,5},{5,4},{6,7},{7,6},{8,9},{9,8},{10,11... | collective-permute-start | bytes 835592 | tf_op jit(solution)/shard_map/ppermute | solution.py:37
  80.1 11.0 %collective-permute-start.33 = (bf16[64,2176]{1,0:T(8,128)(2,1)S(1)}, bf16[64,2176]{1,0:T(8,128)(2,1)S(1)}, u32[]{:S(2)}, u32[]{:S(2)}) collective-permute-start(bf16[64,2176]{1,0:T(8,128)(2,1)S(1)} %collective-permute-done.29.refs_11_.refs_3_), channel_id=1, source_target_pairs={{0,1},{1,0},{2,3},{3,2},{4,5},{5,4},{6,7},{7,6},{8,9},{9,8},{10,11... | collective-permute-start | bytes 835592 | tf_op jit(solution)/shard_map/ppermute | solution.py:37
  83.6 7.5 %collective-permute-start.34 = (bf16[64,2176]{1,0:T(8,128)(2,1)S(1)}, bf16[64,2176]{1,0:T(8,128)(2,1)S(1)}, u32[]{:S(2)}, u32[]{:S(2)}) collective-permute-start(bf16[64,2176]{1,0:T(8,128)(2,1)S(1)} %collective-permute-done.30.refs_12_.refs_4_), channel_id=1, source_target_pairs={{0,1},{1,0},{2,3},{3,2},{4,5},{5,4},{6,7},{7,6},{8,9},{9,8},{10,11... | collective-permute-start | bytes 835592 | tf_op jit(solution)/shard_map/ppermute | solution.py:37
  89.9 9.4 %collective-permute-start.23 = (bf16[64,2048]{1,0:T(8,128)(2,1)}, bf16[64,2048]{1,0:T(8,128)(2,1)S(1)}, u32[]{:S(2)}, u32[]{:S(2)}) collective-permute-start(bf16[64,2048]{1,0:T(8,128)(2,1)} %collective-permute-done.19.refs_1_), channel_id=1, source_target_pairs={{0,1},{1,0},{2,3},{3,2},{4,5},{5,4},{6,7},{7,6},{8,9},{9,8},{10,11... | collective-permute-start | bytes 786440 | tf_op jit(solution)/shard_map/ppermute | solution.py:37
  90.5 9.0 %collective-permute-start.24 = (bf16[64,2048]{1,0:T(8,128)(2,1)S(1)}, bf16[64,2048]{1,0:T(8,128)(2,1)S(1)}, u32[]{:S(2)}, u32[]{:S(2)}) collective-permute-start(bf16[64,2048]{1,0:T(8,128)(2,1)S(1)} %collective-permute-done.20.refs_2_), channel_id=1, source_target_pairs={{0,1},{1,0},{2,3},{3,2},{4,5},{5,4},{6,7},{7,6},{8,9},{9,8},{10,11... | collective-permute-start | bytes 786440 | tf_op jit(solution)/shard_map/ppermute | solution.py:37
  90.6 9.3 %collective-permute-start.25 = (bf16[64,2048]{1,0:T(8,128)(2,1)S(1)}, bf16[64,2048]{1,0:T(8,128)(2,1)S(1)}, u32[]{:S(2)}, u32[]{:S(2)}) collective-permute-start(bf16[64,2048]{1,0:T(8,128)(2,1)S(1)} %collective-permute-done.21.refs_3_), channel_id=1, source_target_pairs={{0,1},{1,0},{2,3},{3,2},{4,5},{5,4},{6,7},{7,6},{8,9},{9,8},{10,11... | collective-permute-start | bytes 786440 | tf_op jit(solution)/shard_map/ppermute | solution.py:37
  91.0 9.0 %collective-permute-start.26 = (bf16[64,2048]{1,0:T(8,128)(2,1)S(1)}, bf16[64,2048]{1,0:T(8,128)(2,1)S(1)}, u32[]{:S(2)}, u32[]{:S(2)}) collective-permute-start(bf16[64,2048]{1,0:T(8,128)(2,1)S(1)} %collective-permute-done.22.refs_4_), channel_id=1, source_target_pairs={{0,1},{1,0},{2,3},{3,2},{4,5},{5,4},{6,7},{7,6},{8,9},{9,8},{10,11... | collective-permute-start | bytes 786440 | tf_op jit(solution)/shard_map/ppermute | solution.py:37
  91.1 15.4 %collective-permute-start.42 = (bf16[128,2048]{1,0:T(8,128)(2,1)S(1)}, bf16[128,2048]{1,0:T(8,128)(2,1)S(1)}, u32[]{:S(2)}, u32[]{:S(2)}) collective-permute-start(bf16[128,2048]{1,0:T(8,128)(2,1)S(1)} %get-tuple-element.29), channel_id=1, source_target_pairs={{0,1},{1,0},{2,3},{3,2},{4,5},{5,4},{6,7},{7,6},{8,9},{9,8},{10,11... | collective-permute-start | bytes 1572872 | tf_op jit(solution)/shard_map/ppermute | solution.py:37
  99.3 11.5 %collective-permute-start.41 = (bf16[128,2048]{1,0:T(8,128)(2,1)S(1)}, bf16[128,2048]{1,0:T(8,128)(2,1)S(1)}, u32[]{:S(2)}, u32[]{:S(2)}) collective-permute-start(bf16[128,2048]{1,0:T(8,128)(2,1)S(1)} %get-tuple-element.27), channel_id=1, source_target_pairs={{0,1},{1,0},{2,3},{3,2},{4,5},{5,4},{6,7},{7,6},{8,9},{9,8},{10,11... | collective-permute-start | bytes 1572872 | tf_op jit(solution)/shard_map/ppermute | solution.py:37
  99.5 7.3 %collective-permute-start.17 = (bf16[128,2048]{1,0:T(8,128)(2,1)S(1)}, bf16[128,2048]{1,0:T(8,128)(2,1)S(1)}, u32[]{:S(2)}, u32[]{:S(2)}) collective-permute-start(bf16[128,2048]{1,0:T(8,128)(2,1)S(1)} %get-tuple-element.21), channel_id=1, source_target_pairs={{0,1},{1,0},{2,3},{3,2},{4,5},{5,4},{6,7},{7,6},{8,9},{9,8},{10,11... | collective-permute-start | bytes 1572872 | tf_op jit(solution)/shard_map/ppermute | solution.py:37
  99.9 24.1 %collective-permute-start.16 = (bf16[128,2048]{1,0:T(8,128)(2,1)S(1)}, bf16[128,2048]{1,0:T(8,128)(2,1)S(1)}, u32[]{:S(2)}, u32[]{:S(2)}) collective-permute-start(bf16[128,2048]{1,0:T(8,128)(2,1)S(1)} %get-tuple-element.19), channel_id=1, source_target_pairs={{0,1},{1,0},{2,3},{3,2},{4,5},{5,4},{6,7},{7,6},{8,9},{9,8},{10,11... | collective-permute-start | bytes 1572872 | tf_op jit(solution)/shard_map/ppermute | solution.py:37
  100.0 7.4 %collective-permute-start.45 = (bf16[128,2048]{1,0:T(8,128)(2,1)S(1)}, bf16[128,2048]{1,0:T(8,128)(2,1)S(1)}, u32[]{:S(2)}, u32[]{:S(2)}) collective-permute-start(bf16[128,2048]{1,0:T(8,128)(2,1)S(1)} %get-tuple-element.33), channel_id=1, source_target_pairs={{0,1},{1,0},{2,3},{3,2},{4,5},{5,4},{6,7},{7,6},{8,9},{9,8},{10,11... | collective-permute-start | bytes 1572872 | tf_op jit(solution)/shard_map/ppermute | solution.py:37
  106.5 28.9 %collective-permute-start.44 = (bf16[128,2048]{1,0:T(8,128)(2,1)S(1)}, bf16[128,2048]{1,0:T(8,128)(2,1)S(1)}, u32[]{:S(2)}, u32[]{:S(2)}) collective-permute-start(bf16[128,2048]{1,0:T(8,128)(2,1)S(1)} %get-tuple-element.31), channel_id=1, source_target_pairs={{0,1},{1,0},{2,3},{3,2},{4,5},{5,4},{6,7},{7,6},{8,9},{9,8},{10,11... | collective-permute-start | bytes 1572872 | tf_op jit(solution)/shard_map/ppermute | solution.py:37
  107.4 14.9 %collective-permute-start.43 = (bf16[128,2048]{1,0:T(8,128)(2,1)S(1)}, bf16[128,2048]{1,0:T(8,128)(2,1)S(1)}, u32[]{:S(2)}, u32[]{:S(2)}) collective-permute-start(bf16[128,2048]{1,0:T(8,128)(2,1)S(1)} %add_convert_fusion.1), channel_id=1, source_target_pairs={{0,2},{1,3},{2,0},{3,1},{4,6},{5,7},{6,4},{7,5},{8,10},{9,11},{10,... | collective-permute-start | bytes 1572872 | tf_op jit(solution)/shard_map/ppermute | solution.py:37
  109.2 24.3 %collective-permute-start.18 = (bf16[128,2048]{1,0:T(8,128)(2,1)S(1)}, bf16[128,2048]{1,0:T(8,128)(2,1)S(1)}, u32[]{:S(2)}, u32[]{:S(2)}) collective-permute-start(bf16[128,2048]{1,0:T(8,128)(2,1)S(1)} %add_convert_fusion.3), channel_id=1, source_target_pairs={{0,2},{1,3},{2,0},{3,1},{4,6},{5,7},{6,4},{7,5},{8,10},{9,11},{10,... | collective-permute-start | bytes 1572872 | tf_op jit(solution)/shard_map/ppermute | solution.py:37
  110.8 35.9 %collective-permute-start.35 = (bf16[128,2048]{1,0:T(8,128)(2,1)S(1)}, bf16[128,2048]{1,0:T(8,128)(2,1)S(1)}, u32[]{:S(2)}, u32[]{:S(2)}) collective-permute-start(bf16[128,2048]{1,0:T(8,128)(2,1)S(1)} %get-tuple-element.23), channel_id=1, source_target_pairs={{0,1},{1,0},{2,3},{3,2},{4,5},{5,4},{6,7},{7,6},{8,9},{9,8},{10,11... | collective-permute-start | bytes 1572872 | tf_op jit(solution)/shard_map/ppermute | solution.py:37
  122.3 22.5 %collective-permute-start.46 = (bf16[128,2048]{1,0:T(8,128)(2,1)S(1)}, bf16[128,2048]{1,0:T(8,128)(2,1)S(1)}, u32[]{:S(2)}, u32[]{:S(2)}) collective-permute-start(bf16[128,2048]{1,0:T(8,128)(2,1)S(1)} %add_convert_fusion), channel_id=1, source_target_pairs={{0,2},{1,3},{2,0},{3,1},{4,6},{5,7},{6,4},{7,5},{8,10},{9,11},{10,... | collective-permute-start | bytes 1572872 | tf_op jit(solution)/shard_map/ppermute | solution.py:37
  124.0 31.1 %collective-permute-start.37 = (bf16[128,2048]{1,0:T(8,128)(2,1)S(1)}, bf16[128,2048]{1,0:T(8,128)(2,1)S(1)}, u32[]{:S(2)}, u32[]{:S(2)}) collective-permute-start(bf16[128,2048]{1,0:T(8,128)(2,1)S(1)} %add_convert_fusion.2), channel_id=1, source_target_pairs={{0,2},{1,3},{2,0},{3,1},{4,6},{5,7},{6,4},{7,5},{8,10},{9,11},{10,... | collective-permute-start | bytes 1572872 | tf_op jit(solution)/shard_map/ppermute | solution.py:37
  133.5 35.6 %collective-permute-start.49 = (bf16[64,2048]{1,0:T(8,128)(2,1)S(1)}, bf16[64,2048]{1,0:T(8,128)(2,1)S(1)}, u32[]{:S(2)}, u32[]{:S(2)}) collective-permute-start(bf16[64,2048]{1,0:T(8,128)(2,1)S(1)} %slice.66), channel_id=1, source_target_pairs={{0,4},{1,5},{2,6},{3,7},{4,0},{5,1},{6,2},{7,3},{8,12},{9,13},{10,... | collective-permute-start | bytes 786440 | tf_op jit(solution)/shard_map/ppermute | solution.py:37
  135.4 43.5 %collective-permute-start.40 = (bf16[64,2048]{1,0:T(8,128)(2,1)S(1)}, bf16[64,2048]{1,0:T(8,128)(2,1)S(1)}, u32[]{:S(2)}, u32[]{:S(2)}) collective-permute-start(bf16[64,2048]{1,0:T(8,128)(2,1)S(1)} %slice.68), channel_id=1, source_target_pairs={{0,4},{1,5},{2,6},{3,7},{4,0},{5,1},{6,2},{7,3},{8,12},{9,13},{10,... | collective-permute-start | bytes 786440 | tf_op jit(solution)/shard_map/ppermute | solution.py:37
  145.0 12.1 %collective-permute-start.47 = (bf16[64,2048]{1,0:T(8,128)(2,1)S(1)}, bf16[64,2048]{1,0:T(8,128)(2,1)S(1)}, u32[]{:S(2)}, u32[]{:S(2)}) collective-permute-start(bf16[64,2048]{1,0:T(8,128)(2,1)S(1)} %slice.67), channel_id=1, source_target_pairs={{0,4},{1,5},{2,6},{3,7},{4,0},{5,1},{6,2},{7,3},{8,12},{9,13},{10,... | collective-permute-start | bytes 786440 | tf_op jit(solution)/shard_map/ppermute | solution.py:37
  155.4 12.8 %collective-permute-start.38 = (bf16[64,2048]{1,0:T(8,128)(2,1)S(1)}, bf16[64,2048]{1,0:T(8,128)(2,1)S(1)}, u32[]{:S(2)}, u32[]{:S(2)}) collective-permute-start(bf16[64,2048]{1,0:T(8,128)(2,1)S(1)} %slice.69), channel_id=1, source_target_pairs={{0,4},{1,5},{2,6},{3,7},{4,0},{5,1},{6,2},{7,3},{8,12},{9,13},{10,... | collective-permute-start | bytes 786440 | tf_op jit(solution)/shard_map/ppermute | solution.py:37
  157.1 20.6 %collective-permute-start.48 = (bf16[64,2048]{1,0:T(8,128)(2,1)S(1)}, bf16[64,2048]{1,0:T(8,128)(2,1)S(1)}, u32[]{:S(2)}, u32[]{:S(2)}) collective-permute-start(bf16[64,2048]{1,0:T(8,128)(2,1)S(1)} %fusion), channel_id=1, source_target_pairs={{0,8},{1,9},{2,10},{3,11},{4,12},{5,13},{6,14},{7,15},{8,0},{9,1},... | collective-permute-start | bytes 786440 | tf_op jit(solution)/shard_map/ppermute | solution.py:37
  168.2 14.8 %collective-permute-start.39 = (bf16[64,2048]{1,0:T(8,128)(2,1)S(1)}, bf16[64,2048]{1,0:T(8,128)(2,1)S(1)}, u32[]{:S(2)}, u32[]{:S(2)}) collective-permute-start(bf16[64,2048]{1,0:T(8,128)(2,1)S(1)} %fusion.2), channel_id=1, source_target_pairs={{0,8},{1,9},{2,10},{3,11},{4,12},{5,13},{6,14},{7,15},{8,0},{9,1},... | collective-permute-start | bytes 786440 | tf_op jit(solution)/shard_map/ppermute | solution.py:37
  (13 other events, 206.8 us)
where the time goes:
time: 184 us
  waiting for transfers between devices  98.8 us (54%)
  starting transfers between devices  44.4 us (24%)
  Pallas kernels  31.6 us (17%)
  other arithmetic  5.95 us (3%)
  local copies, waits for them, and re-layouts  2.17 us (1%)
    ppermute x48, waiting for transfers between devices, swap(): return lax.ppermute(x, 'expert', [(i, i ^ bits) for i in range(self.size)])  93.2 us
    ppermute x48, starting transfers between devices, swap(): return lax.ppermute(x, 'expert', [(i, i ^ bits) for i in range(self.size)])  39.4 us
    pallas_call x2, Pallas kernels, expert_backward(): pl.pallas_call(lambda *refs: backward_kernel(experts, blocks, *refs), out...  15.8 us
    pallas_call x2, Pallas kernels, expert_forward(): pl.pallas_call(lambda *refs: forward_kernel(experts, len(rows), *refs), g...  12.3 us
    ppermute x1, waiting for transfers between devices, from_behind(): return lax.ppermute(block, axis, route)  5.59 us
  transfers between devices with their start and end apart: 50, of which 17 were waited for; matrix products, arithmetic and copies ran while one was open for 3% of the time, Pallas kernels for 17%

commit v1 on v0

--- a/solution.py
+++ b/solution.py
@@ -24,6 +24,9 @@
 
 def inverse_rms(values):
     return lax.rsqrt(jnp.mean(values * values, axis=-1, keepdims=True) + EPSILON)
+
+
+JOINED = (("b", 0), ("b", 1))
 
 
 class Grid:
@@ -56,23 +59,30 @@
             pieces.append(own + other + own_beside + other_beside)
         return pieces
 
-    def scatter_sum(self, partials):
+    def scatter_sum(self, partials, name):
         f32, bf16 = jnp.float32, jnp.bfloat16
         total = {}
-        for group, piece in zip(self.groups, partials):
+        for g, (group, piece) in enumerate(zip(self.groups, partials)):
             own, other, own_beside, other_beside = piece
             other_beside = self.swap(other_beside, 1)
             own_beside = self.swap(own_beside, 1)
             sent = (other.astype(f32) + other_beside.astype(f32)).astype(bf16)
+            block = own.shape[0] // len(group)
+            near = own.astype(f32) + own_beside.astype(f32)
+            if (name, g) in JOINED:
+                joined = self.swap(sent[block:], 4)
+                sent = (sent[:block].astype(f32) + joined.astype(f32)).astype(bf16)
             crossed = self.swap(sent, 2)
-            near = own.astype(f32) + own_beside.astype(f32) + crossed.astype(f32)
-            block = own.shape[0] // len(group)
             for i, k in enumerate(group):
-                total[k] = near[i * block : (i + 1) * block]
+                part = slice(i * block, (i + 1) * block)
+                total[k] = near[part]
+                if part.stop <= crossed.shape[0]:
+                    total[k] = total[k] + crossed[part].astype(f32)
         for k in sorted(total, key=lambda k: (-bin(k).count("1"), -k)):
             low = k & -k
             if k:
-                part = self.swap(total[k].astype(bf16), 4 * low)
+                part = total[k].astype(bf16)
+                part = self.swap(part, 4 * low)
                 total[k - low] = total[k - low] + part.astype(f32)
         return total[0]
 
@@ -314,11 +324,11 @@
         slot_grads.append(
             expert_backward(ids, piece, stored, weights, experts, model_width)
         )
-    grad_normed = grid.scatter_sum(slot_grads)
+    grad_normed = grid.scatter_sum(slot_grads, "b")
     produced = []
     for ids, piece, side in zip(numbers, rows, carried):
         produced.append(expert_forward(ids, piece, side, weights, experts))
-    mixed = inputs_now + grid.scatter_sum(produced)
+    mixed = inputs_now + grid.scatter_sum(produced, "f")
 
     grad_now = gradient_rows(grad_normed, saved_input[0], grad_out, norm_gain)
     return (mixed.astype(bf16)[None], grad_now[None])

time: 184 us -> 172 us (0.935)
  the two profiles are of different devices: /device:TPU:0 before, /device:TPU:15 now
where the time goes in v1:
time: 172 us; the launch traced here: 169 us
  waiting for transfers between devices  91.3 us (53%)
  starting transfers between devices  36.5 us (21%)
  Pallas kernels  31.6 us (18%)
  other arithmetic  5.99 us (3%)
  local copies, waits for them, and re-layouts  2.15 us (1%)
    ppermute x50, waiting for transfers between devices, swap(): return lax.ppermute(x, 'expert', [(i, i ^ bits) for i in range(self.size)])  83.7 us
    ppermute x50, starting transfers between devices, swap(): return lax.ppermute(x, 'expert', [(i, i ^ bits) for i in range(self.size)])  34.9 us
    pallas_call x2, Pallas kernels, expert_backward(): pl.pallas_call(lambda *refs: backward_kernel(experts, blocks, *refs), out...  15.8 us
    pallas_call x2, Pallas kernels, expert_forward(): pl.pallas_call(lambda *refs: forward_kernel(experts, len(rows), *refs), g...  12.3 us
    ppermute x1, waiting for transfers between devices, from_behind(): return lax.ppermute(block, axis, route)  7.63 us
  transfers between devices with their start and end apart: 52, of which 13 were waited for; matrix products, arithmetic and copies ran while one was open for 3% of the time, Pallas kernels for 19%

profile of v1, /device:TPU:15, one launch (start us, length us, event | category | flops | bytes accessed | tf_op | source)
XLA Modules:
  0.0 168.6 jit_solution(6871560051924928442)
XLA Ops:
  0.9 0.8 select_reduce_fusion.2
  1.7 1.1 fusion.12
  2.8 1.3 collective-permute-start
  4.1 0.7 select_reduce_fusion.1
  4.9 0.7 select_reduce_fusion
  6.1 7.6 %collective-permute-done.received = bf16[64,2048]{1,0:T(8,128)(2,1)S(1)} collective-permute-done((bf16[64,2048]{1,0:T(8,128)(2,1)S(1)}, bf16[64,2048]{1,0:T(8,128)(2,1)S(1)}, u32[]{:S(2)}, u32[]{:S(2)}) %collective-permute-start) | collective-permute-done | bytes 262176 | tf_op jit(solution)/shard_map/ppermute | solution.py:17
  13.7 0.9 copy-done.1
  14.7 0.7 copy-done.3
  15.4 0.9 normed_rows.1.refs_1_
  16.3 2.3 %collective-permute-start.19 = (bf16[64,2048]{1,0:T(8,128)(2,1)}, bf16[64,2048]{1,0:T(8,128)(2,1)}, u32[]{:S(2)}, u32[]{:S(2)}) collective-permute-start(bf16[64,2048]{1,0:T(8,128)(2,1)} %normed_rows.1.refs_1_), channel_id=1, source_target_pairs={{0,8},{1,9},{2,10},{3,11},{4,12},{5,13},{6,14},{7,15},{8,0},{9,1},... | collective-permute-start | bytes 786440 | tf_op jit(solution)/shard_map/ppermute | solution.py:40
  19.1 1.3 collective-permute-start.1
  20.4 1.2 collective-permute-start.2
  21.6 8.9 %collective-permute-done.19.refs_1_ = bf16[64,2048]{1,0:T(8,128)(2,1)} collective-permute-done((bf16[64,2048]{1,0:T(8,128)(2,1)}, bf16[64,2048]{1,0:T(8,128)(2,1)}, u32[]{:S(2)}, u32[]{:S(2)}) %collective-permute-start.19) | collective-permute-done | bytes 262176 | tf_op jit(solution)/shard_map/ppermute | solution.py:40
  31.0 4.6 %collective-permute-done.1.refs_2_ = bf16[64,2048]{1,0:T(8,128)(2,1)} collective-permute-done((bf16[64,2048]{1,0:T(8,128)(2,1)}, bf16[64,2048]{1,0:T(8,128)(2,1)}, u32[]{:S(2)}, u32[]{:S(2)}) %collective-permute-start.1) | collective-permute-done | bytes 262176 | tf_op jit(solution)/shard_map/ppermute | solution.py:40
  35.6 2.3 %collective-permute-start.12 = (bf16[64,2176]{1,0:T(8,128)(2,1)S(1)}, bf16[64,2176]{1,0:T(8,128)(2,1)S(1)}, u32[]{:S(2)}, u32[]{:S(2)}) collective-permute-start(bf16[64,2176]{1,0:T(8,128)(2,1)S(1)} %pad_maximum_fusion.refs_9_.refs_1_), channel_id=1, source_target_pairs={{0,1},{1,0},{2,3},{3,2},{4,5},{5,4},{6,7},{7,6},{8,9},{9,8},{10,11... | collective-permute-start | bytes 835592 | tf_op jit(solution)/shard_map/ppermute | solution.py:40
  37.9 1.2 collective-permute-start.27
  39.6 1.2 collective-permute-start.11
  41.1 10.3 %collective-permute-done.27.refs_9_.refs_1_ = bf16[64,2176]{1,0:T(8,128)(2,1)S(1)} collective-permute-done((bf16[64,2176]{1,0:T(8,128)(2,1)S(1)}, bf16[64,2176]{1,0:T(8,128)(2,1)S(1)}, u32[]{:S(2)}, u32[]{:S(2)}) %collective-permute-start.27) | collective-permute-done | bytes 278560 | tf_op jit(solution)/shard_map/ppermute | solution.py:40
  51.9 0.6 collective-permute-start.14
  52.6 1.6 collective-permute-start.28
  54.2 1.1 collective-permute-start.15
  55.2 1.5 prepare.1.refs_9_
  56.7 1.7 collective-permute-done.3.refs_4_
  58.4 1.4 collective-permute-start.5
  60.2 0.6 collective-permute-done.28.refs_10_.refs_2_
  60.7 1.0 collective-permute-start.7
  62.1 8.0 %expert_backward.2 = (bf16[128,2048]{1,0:T(8,128)(2,1)S(1)}, bf16[128,2048]{1,0:T(8,128)(2,1)S(1)}, bf16[128,2048]{1,0:T(8,128)(2,1)S(1)}, bf16[128,2048]{1,0:T(8,128)(2,1)S(1)}) custom-call(s32[9]{0:T(128)S(1)} %broadcast_xor_fusion.1.refs_0_, bf16[64,2176]{1,0:T(8,128)(2,1)S(1)} %pad_maximum_fusion.refs_9_.refs_1_, ...), custom_call_target="tpu_custom_call" | custom-call | flops 4831838208 | bytes 12582912 | tf_op jit(solution)/shard_map/expert_backward/pallas_call | solution.py:214
  70.6 1.1 collective-permute-start.22
  71.6 0.5 collective-permute-start.32
  72.2 1.4 collective-permute-done.30.refs_12_.refs_4_
  73.6 2.2 %collective-permute-start.34 = (bf16[64,2176]{1,0:T(8,128)(2,1)S(1)}, bf16[64,2176]{1,0:T(8,128)(2,1)S(1)}, u32[]{:S(2)}, u32[]{:S(2)}) collective-permute-start(bf16[64,2176]{1,0:T(8,128)(2,1)S(1)} %collective-permute-done.30.refs_12_.refs_4_), channel_id=1, source_target_pairs={{0,1},{1,0},{2,3},{3,2},{4,5},{5,4},{6,7},{7,6},{8,9},{9,8},{10,11... | collective-permute-start | bytes 835592 | tf_op jit(solution)/shard_map/ppermute | solution.py:40
  75.8 6.3 %expert_forward.2 = (bf16[128,2048]{1,0:T(8,128)(2,1)S(1)}, bf16[128,2048]{1,0:T(8,128)(2,1)S(1)}, bf16[128,2048]{1,0:T(8,128)(2,1)S(1)}, bf16[128,2048]{1,0:T(8,128)(2,1)S(1)}) custom-call(s32[9]{0:T(128)S(1)} %broadcast_xor_fusion.1.refs_0_, bf16[64,2048]{1,0:T(8,128)(2,1)} %normed_rows.1.refs_1_, bf16[64,2048]{1,0:T(8,128)(2,1)} %collective-permute-done.1.refs_2_, ...), custom_call_target="tpu_custom_call" | custom-call | flops 4831838208 | bytes 10485760 | tf_op jit(solution)/shard_map/expert_forward/pallas_call | solution.py:196
  83.3 7.7 %expert_backward.3 = (bf16[128,2048]{1,0:T(8,128)(2,1)S(1)}, bf16[128,2048]{1,0:T(8,128)(2,1)S(1)}, bf16[128,2048]{1,0:T(8,128)(2,1)S(1)}, bf16[128,2048]{1,0:T(8,128)(2,1)S(1)}) custom-call(s32[9]{0:T(128)S(1)} %broadcast_xor_fusion.refs_0_, bf16[64,2176]{1,0:T(8,128)(2,1)S(1)} %collective-permute-done.27.refs_9_.refs_1_, ...), custom_call_target="tpu_custom_call" | custom-call | flops 4831838208 | bytes 12582912 | tf_op jit(solution)/shard_map/expert_backward/pallas_call | solution.py:214
  92.2 6.0 %expert_forward.3 = (bf16[128,2048]{1,0:T(8,128)(2,1)S(1)}, bf16[128,2048]{1,0:T(8,128)(2,1)S(1)}, bf16[128,2048]{1,0:T(8,128)(2,1)S(1)}, bf16[128,2048]{1,0:T(8,128)(2,1)S(1)}) custom-call(s32[9]{0:T(128)S(1)} %broadcast_xor_fusion.refs_0_, bf16[64,2048]{1,0:T(8,128)(2,1)} %collective-permute-done.19.refs_1_, ...), custom_call_target="tpu_custom_call" | custom-call | flops 4831838208 | bytes 10485760 | tf_op jit(solution)/shard_map/expert_forward/pallas_call | solution.py:196
  99.9 1.4 collective-permute-start.43
  101.4 6.3 %collective-permute-done.43 = bf16[64,2048]{1,0:T(8,128)(2,1)S(1)} collective-permute-done((bf16[64,2048]{1,0:T(8,128)(2,1)S(1)}, bf16[64,2048]{1,0:T(8,128)(2,1)S(1)}, u32[]{:S(2)}, u32[]{:S(2)}) %collective-permute-start.43) | collective-permute-done | bytes 262176 | tf_op jit(solution)/shard_map/ppermute | solution.py:40
  107.7 1.3 collective-permute-start.51
  109.3 1.5 collective-permute-start.44
  111.4 1.4 collective-permute-start.49
  112.9 8.5 %collective-permute-done.18 = bf16[128,2048]{1,0:T(8,128)(2,1)S(1)} collective-permute-done((bf16[128,2048]{1,0:T(8,128)(2,1)S(1)}, bf16[128,2048]{1,0:T(8,128)(2,1)S(1)}, u32[]{:S(2)}, u32[]{:S(2)}) %collective-permute-start.18) | collective-permute-done | bytes 524320 | tf_op jit(solution)/shard_map/ppermute | solution.py:40
  122.0 16.3 %collective-permute-done.37 = bf16[128,2048]{1,0:T(8,128)(2,1)S(1)} collective-permute-done((bf16[128,2048]{1,0:T(8,128)(2,1)S(1)}, bf16[128,2048]{1,0:T(8,128)(2,1)S(1)}, u32[]{:S(2)}, u32[]{:S(2)}) %collective-permute-start.37) | collective-permute-done | bytes 524320 | tf_op jit(solution)/shard_map/ppermute | solution.py:40
  138.8 5.3 %collective-permute-done.48 = bf16[64,2048]{1,0:T(8,128)(2,1)S(1)} collective-permute-done((bf16[64,2048]{1,0:T(8,128)(2,1)S(1)}, bf16[64,2048]{1,0:T(8,128)(2,1)S(1)}, u32[]{:S(2)}, u32[]{:S(2)}) %collective-permute-start.48) | collective-permute-done | bytes 262176 | tf_op jit(solution)/shard_map/ppermute | solution.py:40
  144.1 1.2 collective-permute-start.50
  145.5 1.3 collective-permute-start.39
  146.7 15.3 %collective-permute-done.50 = bf16[64,2048]{1,0:T(8,128)(2,1)S(1)} collective-permute-done((bf16[64,2048]{1,0:T(8,128)(2,1)S(1)}, bf16[64,2048]{1,0:T(8,128)(2,1)S(1)}, u32[]{:S(2)}, u32[]{:S(2)}) %collective-permute-start.50) | collective-permute-done | bytes 262176 | tf_op jit(solution)/shard_map/ppermute | solution.py:40
  162.2 1.1 gradient_rows.1
  163.3 4.4 %collective-permute-done.39 = bf16[64,2048]{1,0:T(8,128)(2,1)S(1)} collective-permute-done((bf16[64,2048]{1,0:T(8,128)(2,1)S(1)}, bf16[64,2048]{1,0:T(8,128)(2,1)S(1)}, u32[]{:S(2)}, u32[]{:S(2)}) %collective-permute-start.39) | collective-permute-done | bytes 262176 | tf_op jit(solution)/shard_map/ppermute | solution.py:40
  167.7 0.9 fusion.13
  (121 shorter events, 10.4 us)
Async XLA Ops:
  0.6 17.9 %collective-permute-start.8 = (bf16[64,2048]{1,0:T(8,128)(2,1)}, bf16[64,2048]{1,0:T(8,128)(2,1)S(1)}, u32[]{:S(2)}, u32[]{:S(2)}) collective-permute-start(bf16[64,2048]{1,0:T(8,128)(2,1)} %bitcast.40), channel_id=1, source_target_pairs={{0,16},{16,0},{1,17},{17,1},{2,18},{18,2},{3,19},{19,3},{4,20},{20... | collective-permute-start | bytes 786440 | tf_op jit(solution)/shard_map/ppermute | solution.py:22
  2.8 10.9 %collective-permute-start = (bf16[64,2048]{1,0:T(8,128)(2,1)S(1)}, bf16[64,2048]{1,0:T(8,128)(2,1)S(1)}, u32[]{:S(2)}, u32[]{:S(2)}) collective-permute-start(bf16[64,2048]{1,0:T(8,128)(2,1)S(1)} %fusion.12), channel_id=1, source_target_pairs={{0,16},{1,17},{2,18},{3,19},{4,20},{5,21},{6,22},{7,23},{8,24},{9,... | collective-permute-start | bytes 786440 | tf_op jit(solution)/shard_map/ppermute | solution.py:17
  16.3 14.2 %collective-permute-start.19 = (bf16[64,2048]{1,0:T(8,128)(2,1)}, bf16[64,2048]{1,0:T(8,128)(2,1)}, u32[]{:S(2)}, u32[]{:S(2)}) collective-permute-start(bf16[64,2048]{1,0:T(8,128)(2,1)} %normed_rows.1.refs_1_), channel_id=1, source_target_pairs={{0,8},{1,9},{2,10},{3,11},{4,12},{5,13},{6,14},{7,15},{8,0},{9,1},... | collective-permute-start | bytes 786440 | tf_op jit(solution)/shard_map/ppermute | solution.py:40
  18.6 20.7 %collective-permute-start.9 = (bf16[64,2176]{1,0:T(8,128)(2,1)S(1)}, bf16[64,2176]{1,0:T(8,128)(2,1)S(1)}, u32[]{:S(2)}, u32[]{:S(2)}) collective-permute-start(bf16[64,2176]{1,0:T(8,128)(2,1)S(1)} %pad_maximum_fusion.refs_9_.refs_1_), channel_id=1, source_target_pairs={{0,4},{1,5},{2,6},{3,7},{4,0},{5,1},{6,2},{7,3},{8,12},{9,13},{10,... | collective-permute-start | bytes 835592 | tf_op jit(solution)/shard_map/ppermute | solution.py:40
  18.8 20.7 %collective-permute-start.10 = (bf16[64,2176]{1,0:T(8,128)(2,1)S(1)}, bf16[64,2176]{1,0:T(8,128)(2,1)}, u32[]{:S(2)}, u32[]{:S(2)}) collective-permute-start(bf16[64,2176]{1,0:T(8,128)(2,1)S(1)} %pad_maximum_fusion.refs_9_.refs_1_), channel_id=1, source_target_pairs={{0,2},{1,3},{2,0},{3,1},{4,6},{5,7},{6,4},{7,5},{8,10},{9,11},{10,... | collective-permute-start | bytes 835592 | tf_op jit(solution)/shard_map/ppermute | solution.py:40
  19.1 16.5 %collective-permute-start.1 = (bf16[64,2048]{1,0:T(8,128)(2,1)}, bf16[64,2048]{1,0:T(8,128)(2,1)}, u32[]{:S(2)}, u32[]{:S(2)}) collective-permute-start(bf16[64,2048]{1,0:T(8,128)(2,1)} %normed_rows.1.refs_1_), channel_id=1, source_target_pairs={{0,4},{1,5},{2,6},{3,7},{4,0},{5,1},{6,2},{7,3},{8,12},{9,13},{10,... | collective-permute-start | bytes 786440 | tf_op jit(solution)/shard_map/ppermute | solution.py:40
  20.4 17.6 %collective-permute-start.2 = (bf16[64,2048]{1,0:T(8,128)(2,1)}, bf16[64,2048]{1,0:T(8,128)(2,1)}, u32[]{:S(2)}, u32[]{:S(2)}) collective-permute-start(bf16[64,2048]{1,0:T(8,128)(2,1)} %normed_rows.1.refs_1_), channel_id=1, source_target_pairs={{0,2},{1,3},{2,0},{3,1},{4,6},{5,7},{6,4},{7,5},{8,10},{9,11},{10,... | collective-permute-start | bytes 786440 | tf_op jit(solution)/shard_map/ppermute | solution.py:40
  30.5 8.7 %collective-permute-start.4 = (bf16[64,2048]{1,0:T(8,128)(2,1)}, bf16[64,2048]{1,0:T(8,128)(2,1)}, u32[]{:S(2)}, u32[]{:S(2)}) collective-permute-start(bf16[64,2048]{1,0:T(8,128)(2,1)} %normed_rows.1.refs_1_), channel_id=1, source_target_pairs={{0,1},{1,0},{2,3},{3,2},{4,5},{5,4},{6,7},{7,6},{8,9},{9,8},{10,11... | collective-permute-start | bytes 786440 | tf_op jit(solution)/shard_map/ppermute | solution.py:40
  37.9 13.5 %collective-permute-start.27 = (bf16[64,2176]{1,0:T(8,128)(2,1)S(1)}, bf16[64,2176]{1,0:T(8,128)(2,1)S(1)}, u32[]{:S(2)}, u32[]{:S(2)}) collective-permute-start(bf16[64,2176]{1,0:T(8,128)(2,1)S(1)} %pad_maximum_fusion.refs_9_.refs_1_), channel_id=1, source_target_pairs={{0,8},{1,9},{2,10},{3,11},{4,12},{5,13},{6,14},{7,15},{8,0},{9,1},... | collective-permute-start | bytes 835592 | tf_op jit(solution)/shard_map/ppermute | solution.py:40
  39.1 12.8 %collective-permute-start.20 = (bf16[64,2048]{1,0:T(8,128)(2,1)}, bf16[64,2048]{1,0:T(8,128)(2,1)S(1)}, u32[]{:S(2)}, u32[]{:S(2)}) collective-permute-start(bf16[64,2048]{1,0:T(8,128)(2,1)} %collective-permute-done.19.refs_1_), channel_id=1, source_target_pairs={{0,4},{1,5},{2,6},{3,7},{4,0},{5,1},{6,2},{7,3},{8,12},{9,13},{10,... | collective-permute-start | bytes 786440 | tf_op jit(solution)/shard_map/ppermute | solution.py:40
  39.3 13.3 %collective-permute-start.21 = (bf16[64,2048]{1,0:T(8,128)(2,1)}, bf16[64,2048]{1,0:T(8,128)(2,1)S(1)}, u32[]{:S(2)}, u32[]{:S(2)}) collective-permute-start(bf16[64,2048]{1,0:T(8,128)(2,1)} %collective-permute-done.19.refs_1_), channel_id=1, source_target_pairs={{0,2},{1,3},{2,0},{3,1},{4,6},{5,7},{6,4},{7,5},{8,10},{9,11},{10,... | collective-permute-start | bytes 786440 | tf_op jit(solution)/shard_map/ppermute | solution.py:40
  39.6 14.6 %collective-permute-start.11 = (bf16[64,2176]{1,0:T(8,128)(2,1)S(1)}, bf16[64,2176]{1,0:T(8,128)(2,1)S(1)}, u32[]{:S(2)}, u32[]{:S(2)}) collective-permute-start(bf16[64,2176]{1,0:T(8,128)(2,1)S(1)} %collective-permute-done.9.refs_10_.refs_2_), channel_id=1, source_target_pairs={{0,2},{1,3},{2,0},{3,1},{4,6},{5,7},{6,4},{7,5},{8,10},{9,11},{10,... | collective-permute-start | bytes 835592 | tf_op jit(solution)/shard_map/ppermute | solution.py:40
  40.9 17.5 %collective-permute-start.3 = (bf16[64,2048]{1,0:T(8,128)(2,1)}, bf16[64,2048]{1,0:T(8,128)(2,1)S(1)}, u32[]{:S(2)}, u32[]{:S(2)}) collective-permute-start(bf16[64,2048]{1,0:T(8,128)(2,1)} %collective-permute-done.1.refs_2_), channel_id=1, source_target_pairs={{0,2},{1,3},{2,0},{3,1},{4,6},{5,7},{6,4},{7,5},{8,10},{9,11},{10,... | collective-permute-start | bytes 786440 | tf_op jit(solution)/shard_map/ppermute | solution.py:40
  51.5 8.4 %collective-permute-start.13 = (bf16[64,2176]{1,0:T(8,128)(2,1)S(1)}, bf16[64,2176]{1,0:T(8,128)(2,1)S(1)}, u32[]{:S(2)}, u32[]{:S(2)}) collective-permute-start(bf16[64,2176]{1,0:T(8,128)(2,1)S(1)} %collective-permute-done.9.refs_10_.refs_2_), channel_id=1, source_target_pairs={{0,1},{1,0},{2,3},{3,2},{4,5},{5,4},{6,7},{7,6},{8,9},{9,8},{10,11... | collective-permute-start | bytes 835592 | tf_op jit(solution)/shard_map/ppermute | solution.py:40
  51.9 7.9 %collective-permute-start.14 = (bf16[64,2176]{1,0:T(8,128)(2,1)}, bf16[64,2176]{1,0:T(8,128)(2,1)S(1)}, u32[]{:S(2)}, u32[]{:S(2)}) collective-permute-start(bf16[64,2176]{1,0:T(8,128)(2,1)} %collective-permute-done.10.refs_11_.refs_3_), channel_id=1, source_target_pairs={{0,1},{1,0},{2,3},{3,2},{4,5},{5,4},{6,7},{7,6},{8,9},{9,8},{10,11... | collective-permute-start | bytes 835592 | tf_op jit(solution)/shard_map/ppermute | solution.py:40
  52.6 8.2 %collective-permute-start.28 = (bf16[64,2176]{1,0:T(8,128)(2,1)S(1)}, bf16[64,2176]{1,0:T(8,128)(2,1)S(1)}, u32[]{:S(2)}, u32[]{:S(2)}) collective-permute-start(bf16[64,2176]{1,0:T(8,128)(2,1)S(1)} %collective-permute-done.27.refs_9_.refs_1_), channel_id=1, source_target_pairs={{0,4},{1,5},{2,6},{3,7},{4,0},{5,1},{6,2},{7,3},{8,12},{9,13},{10,... | collective-permute-start | bytes 835592 | tf_op jit(solution)/shard_map/ppermute | solution.py:40
  54.2 7.6 %collective-permute-start.15 = (bf16[64,2176]{1,0:T(8,128)(2,1)S(1)}, bf16[64,2176]{1,0:T(8,128)(2,1)S(1)}, u32[]{:S(2)}, u32[]{:S(2)}) collective-permute-start(bf16[64,2176]{1,0:T(8,128)(2,1)S(1)} %collective-permute-done.11.refs_12_.refs_4_), channel_id=1, source_target_pairs={{0,1},{1,0},{2,3},{3,2},{4,5},{5,4},{6,7},{7,6},{8,9},{9,8},{10,11... | collective-permute-start | bytes 835592 | tf_op jit(solution)/shard_map/ppermute | solution.py:40
  58.4 11.7 %collective-permute-start.5 = (bf16[64,2048]{1,0:T(8,128)(2,1)}, bf16[64,2048]{1,0:T(8,128)(2,1)S(1)}, u32[]{:S(2)}, u32[]{:S(2)}) collective-permute-start(bf16[64,2048]{1,0:T(8,128)(2,1)} %collective-permute-done.1.refs_2_), channel_id=1, source_target_pairs={{0,1},{1,0},{2,3},{3,2},{4,5},{5,4},{6,7},{7,6},{8,9},{9,8},{10,11... | collective-permute-start | bytes 786440 | tf_op jit(solution)/shard_map/ppermute | solution.py:40
  59.8 10.7 %collective-permute-start.6 = (bf16[64,2048]{1,0:T(8,128)(2,1)}, bf16[64,2048]{1,0:T(8,128)(2,1)S(1)}, u32[]{:S(2)}, u32[]{:S(2)}) collective-permute-start(bf16[64,2048]{1,0:T(8,128)(2,1)} %collective-permute-done.2.refs_3_), channel_id=1, source_target_pairs={{0,1},{1,0},{2,3},{3,2},{4,5},{5,4},{6,7},{7,6},{8,9},{9,8},{10,11... | collective-permute-start | bytes 786440 | tf_op jit(solution)/shard_map/ppermute | solution.py:40
  59.8 11.8 %collective-permute-start.29 = (bf16[64,2176]{1,0:T(8,128)(2,1)S(1)}, bf16[64,2176]{1,0:T(8,128)(2,1)S(1)}, u32[]{:S(2)}, u32[]{:S(2)}) collective-permute-start(bf16[64,2176]{1,0:T(8,128)(2,1)S(1)} %collective-permute-done.27.refs_9_.refs_1_), channel_id=1, source_target_pairs={{0,2},{1,3},{2,0},{3,1},{4,6},{5,7},{6,4},{7,5},{8,10},{9,11},{10,... | collective-permute-start | bytes 835592 | tf_op jit(solution)/shard_map/ppermute | solution.py:40
  60.7 11.4 %collective-permute-start.7 = (bf16[64,2048]{1,0:T(8,128)(2,1)S(1)}, bf16[64,2048]{1,0:T(8,128)(2,1)S(1)}, u32[]{:S(2)}, u32[]{:S(2)}) collective-permute-start(bf16[64,2048]{1,0:T(8,128)(2,1)S(1)} %collective-permute-done.3.refs_4_), channel_id=1, source_target_pairs={{0,1},{1,0},{2,3},{3,2},{4,5},{5,4},{6,7},{7,6},{8,9},{9,8},{10,11... | collective-permute-start | bytes 786440 | tf_op jit(solution)/shard_map/ppermute | solution.py:40
  61.8 11.9 %collective-permute-start.30 = (bf16[64,2176]{1,0:T(8,128)(2,1)S(1)}, bf16[64,2176]{1,0:T(8,128)(2,1)S(1)}, u32[]{:S(2)}, u32[]{:S(2)}) collective-permute-start(bf16[64,2176]{1,0:T(8,128)(2,1)S(1)} %collective-permute-done.28.refs_10_.refs_2_), channel_id=1, source_target_pairs={{0,2},{1,3},{2,0},{3,1},{4,6},{5,7},{6,4},{7,5},{8,10},{9,11},{10,... | collective-permute-start | bytes 835592 | tf_op jit(solution)/shard_map/ppermute | solution.py:40
  70.1 12.0 %collective-permute-start.31 = (bf16[64,2176]{1,0:T(8,128)(2,1)S(1)}, bf16[64,2176]{1,0:T(8,128)(2,1)S(1)}, u32[]{:S(2)}, u32[]{:S(2)}) collective-permute-start(bf16[64,2176]{1,0:T(8,128)(2,1)S(1)} %collective-permute-done.27.refs_9_.refs_1_), channel_id=1, source_target_pairs={{0,1},{1,0},{2,3},{3,2},{4,5},{5,4},{6,7},{7,6},{8,9},{9,8},{10,11... | collective-permute-start | bytes 835592 | tf_op jit(solution)/shard_map/ppermute | solution.py:40
  70.6 11.7 %collective-permute-start.22 = (bf16[64,2048]{1,0:T(8,128)(2,1)S(1)}, bf16[64,2048]{1,0:T(8,128)(2,1)S(1)}, u32[]{:S(2)}, u32[]{:S(2)}) collective-permute-start(bf16[64,2048]{1,0:T(8,128)(2,1)S(1)} %collective-permute-done.20.refs_2_), channel_id=1, source_target_pairs={{0,2},{1,3},{2,0},{3,1},{4,6},{5,7},{6,4},{7,5},{8,10},{9,11},{10,... | collective-permute-start | bytes 786440 | tf_op jit(solution)/shard_map/ppermute | solution.py:40
  71.6 11.1 %collective-permute-start.32 = (bf16[64,2176]{1,0:T(8,128)(2,1)S(1)}, bf16[64,2176]{1,0:T(8,128)(2,1)S(1)}, u32[]{:S(2)}, u32[]{:S(2)}) collective-permute-start(bf16[64,2176]{1,0:T(8,128)(2,1)S(1)} %collective-permute-done.28.refs_10_.refs_2_), channel_id=1, source_target_pairs={{0,1},{1,0},{2,3},{3,2},{4,5},{5,4},{6,7},{7,6},{8,9},{9,8},{10,11... | collective-permute-start | bytes 835592 | tf_op jit(solution)/shard_map/ppermute | solution.py:40
  72.2 10.7 %collective-permute-start.33 = (bf16[64,2176]{1,0:T(8,128)(2,1)S(1)}, bf16[64,2176]{1,0:T(8,128)(2,1)S(1)}, u32[]{:S(2)}, u32[]{:S(2)}) collective-permute-start(bf16[64,2176]{1,0:T(8,128)(2,1)S(1)} %collective-permute-done.29.refs_11_.refs_3_), channel_id=1, source_target_pairs={{0,1},{1,0},{2,3},{3,2},{4,5},{5,4},{6,7},{7,6},{8,9},{9,8},{10,11... | collective-permute-start | bytes 835592 | tf_op jit(solution)/shard_map/ppermute | solution.py:40
  73.6 9.6 %collective-permute-start.34 = (bf16[64,2176]{1,0:T(8,128)(2,1)S(1)}, bf16[64,2176]{1,0:T(8,128)(2,1)S(1)}, u32[]{:S(2)}, u32[]{:S(2)}) collective-permute-start(bf16[64,2176]{1,0:T(8,128)(2,1)S(1)} %collective-permute-done.30.refs_12_.refs_4_), channel_id=1, source_target_pairs={{0,1},{1,0},{2,3},{3,2},{4,5},{5,4},{6,7},{7,6},{8,9},{9,8},{10,11... | collective-permute-start | bytes 835592 | tf_op jit(solution)/shard_map/ppermute | solution.py:40
  82.2 8.9 %collective-permute-start.23 = (bf16[64,2048]{1,0:T(8,128)(2,1)}, bf16[64,2048]{1,0:T(8,128)(2,1)S(1)}, u32[]{:S(2)}, u32[]{:S(2)}) collective-permute-start(bf16[64,2048]{1,0:T(8,128)(2,1)} %collective-permute-done.19.refs_1_), channel_id=1, source_target_pairs={{0,1},{1,0},{2,3},{3,2},{4,5},{5,4},{6,7},{7,6},{8,9},{9,8},{10,11... | collective-permute-start | bytes 786440 | tf_op jit(solution)/shard_map/ppermute | solution.py:40
  82.2 9.4 %collective-permute-start.24 = (bf16[64,2048]{1,0:T(8,128)(2,1)S(1)}, bf16[64,2048]{1,0:T(8,128)(2,1)S(1)}, u32[]{:S(2)}, u32[]{:S(2)}) collective-permute-start(bf16[64,2048]{1,0:T(8,128)(2,1)S(1)} %collective-permute-done.20.refs_2_), channel_id=1, source_target_pairs={{0,1},{1,0},{2,3},{3,2},{4,5},{5,4},{6,7},{7,6},{8,9},{9,8},{10,11... | collective-permute-start | bytes 786440 | tf_op jit(solution)/shard_map/ppermute | solution.py:40
  82.7 9.0 %collective-permute-start.25 = (bf16[64,2048]{1,0:T(8,128)(2,1)S(1)}, bf16[64,2048]{1,0:T(8,128)(2,1)S(1)}, u32[]{:S(2)}, u32[]{:S(2)}) collective-permute-start(bf16[64,2048]{1,0:T(8,128)(2,1)S(1)} %collective-permute-done.21.refs_3_), channel_id=1, source_target_pairs={{0,1},{1,0},{2,3},{3,2},{4,5},{5,4},{6,7},{7,6},{8,9},{9,8},{10,11... | collective-permute-start | bytes 786440 | tf_op jit(solution)/shard_map/ppermute | solution.py:40
  82.8 9.3 %collective-permute-start.26 = (bf16[64,2048]{1,0:T(8,128)(2,1)S(1)}, bf16[64,2048]{1,0:T(8,128)(2,1)S(1)}, u32[]{:S(2)}, u32[]{:S(2)}) collective-permute-start(bf16[64,2048]{1,0:T(8,128)(2,1)S(1)} %collective-permute-done.22.refs_4_), channel_id=1, source_target_pairs={{0,1},{1,0},{2,3},{3,2},{4,5},{5,4},{6,7},{7,6},{8,9},{9,8},{10,11... | collective-permute-start | bytes 786440 | tf_op jit(solution)/shard_map/ppermute | solution.py:40
  83.3 15.0 %collective-permute-start.41 = (bf16[128,2048]{1,0:T(8,128)(2,1)S(1)}, bf16[128,2048]{1,0:T(8,128)(2,1)S(1)}, u32[]{:S(2)}, u32[]{:S(2)}) collective-permute-start(bf16[128,2048]{1,0:T(8,128)(2,1)S(1)} %get-tuple-element.27), channel_id=1, source_target_pairs={{0,1},{1,0},{2,3},{3,2},{4,5},{5,4},{6,7},{7,6},{8,9},{9,8},{10,11... | collective-permute-start | bytes 1572872 | tf_op jit(solution)/shard_map/ppermute | solution.py:40
  91.1 7.8 %collective-permute-start.42 = (bf16[128,2048]{1,0:T(8,128)(2,1)S(1)}, bf16[128,2048]{1,0:T(8,128)(2,1)S(1)}, u32[]{:S(2)}, u32[]{:S(2)}) collective-permute-start(bf16[128,2048]{1,0:T(8,128)(2,1)S(1)} %get-tuple-element.29), channel_id=1, source_target_pairs={{0,1},{1,0},{2,3},{3,2},{4,5},{5,4},{6,7},{7,6},{8,9},{9,8},{10,11... | collective-permute-start | bytes 1572872 | tf_op jit(solution)/shard_map/ppermute | solution.py:40
  91.6 8.3 %collective-permute-start.17 = (bf16[128,2048]{1,0:T(8,128)(2,1)S(1)}, bf16[128,2048]{1,0:T(8,128)(2,1)S(1)}, u32[]{:S(2)}, u32[]{:S(2)}) collective-permute-start(bf16[128,2048]{1,0:T(8,128)(2,1)S(1)} %get-tuple-element.21), channel_id=1, source_target_pairs={{0,1},{1,0},{2,3},{3,2},{4,5},{5,4},{6,7},{7,6},{8,9},{9,8},{10,11... | collective-permute-start | bytes 1572872 | tf_op jit(solution)/shard_map/ppermute | solution.py:40
  92.1 17.2 %collective-permute-start.46 = (bf16[128,2048]{1,0:T(8,128)(2,1)S(1)}, bf16[128,2048]{1,0:T(8,128)(2,1)S(1)}, u32[]{:S(2)}, u32[]{:S(2)}) collective-permute-start(bf16[128,2048]{1,0:T(8,128)(2,1)S(1)} %get-tuple-element.33), channel_id=1, source_target_pairs={{0,1},{1,0},{2,3},{3,2},{4,5},{5,4},{6,7},{7,6},{8,9},{9,8},{10,11... | collective-permute-start | bytes 1572872 | tf_op jit(solution)/shard_map/ppermute | solution.py:40
  98.3 10.8 %collective-permute-start.45 = (bf16[128,2048]{1,0:T(8,128)(2,1)S(1)}, bf16[128,2048]{1,0:T(8,128)(2,1)S(1)}, u32[]{:S(2)}, u32[]{:S(2)}) collective-permute-start(bf16[128,2048]{1,0:T(8,128)(2,1)S(1)} %get-tuple-element.31), channel_id=1, source_target_pairs={{0,1},{1,0},{2,3},{3,2},{4,5},{5,4},{6,7},{7,6},{8,9},{9,8},{10,11... | collective-permute-start | bytes 1572872 | tf_op jit(solution)/shard_map/ppermute | solution.py:40
  98.9 12.1 %collective-permute-start.36 = (bf16[128,2048]{1,0:T(8,128)(2,1)S(1)}, bf16[128,2048]{1,0:T(8,128)(2,1)S(1)}, u32[]{:S(2)}, u32[]{:S(2)}) collective-permute-start(bf16[128,2048]{1,0:T(8,128)(2,1)S(1)} %get-tuple-element.25), channel_id=1, source_target_pairs={{0,1},{1,0},{2,3},{3,2},{4,5},{5,4},{6,7},{7,6},{8,9},{9,8},{10,11... | collective-permute-start | bytes 1572872 | tf_op jit(solution)/shard_map/ppermute | solution.py:40
  99.2 12.2 %collective-permute-start.35 = (bf16[128,2048]{1,0:T(8,128)(2,1)S(1)}, bf16[128,2048]{1,0:T(8,128)(2,1)S(1)}, u32[]{:S(2)}, u32[]{:S(2)}) collective-permute-start(bf16[128,2048]{1,0:T(8,128)(2,1)S(1)} %get-tuple-element.23), channel_id=1, source_target_pairs={{0,1},{1,0},{2,3},{3,2},{4,5},{5,4},{6,7},{7,6},{8,9},{9,8},{10,11... | collective-permute-start | bytes 1572872 | tf_op jit(solution)/shard_map/ppermute | solution.py:40
  99.9 7.8 %collective-permute-start.43 = (bf16[64,2048]{1,0:T(8,128)(2,1)S(1)}, bf16[64,2048]{1,0:T(8,128)(2,1)S(1)}, u32[]{:S(2)}, u32[]{:S(2)}) collective-permute-start(bf16[64,2048]{1,0:T(8,128)(2,1)S(1)} %slice.76), channel_id=1, source_target_pairs={{0,4},{1,5},{2,6},{3,7},{4,0},{5,1},{6,2},{7,3},{8,12},{9,13},{10,... | collective-permute-start | bytes 786440 | tf_op jit(solution)/shard_map/ppermute | solution.py:40
  107.7 39.0 %collective-permute-start.51 = (bf16[64,2048]{1,0:T(8,128)(2,1)S(1)}, bf16[64,2048]{1,0:T(8,128)(2,1)S(1)}, u32[]{:S(2)}, u32[]{:S(2)}) collective-permute-start(bf16[64,2048]{1,0:T(8,128)(2,1)S(1)} %slice.122), channel_id=1, source_target_pairs={{0,4},{1,5},{2,6},{3,7},{4,0},{5,1},{6,2},{7,3},{8,12},{9,13},{10,... | collective-permute-start | bytes 786440 | tf_op jit(solution)/shard_map/ppermute | solution.py:40
  109.1 12.3 %collective-permute-start.18 = (bf16[128,2048]{1,0:T(8,128)(2,1)S(1)}, bf16[128,2048]{1,0:T(8,128)(2,1)S(1)}, u32[]{:S(2)}, u32[]{:S(2)}) collective-permute-start(bf16[128,2048]{1,0:T(8,128)(2,1)S(1)} %add_convert_fusion.3), channel_id=1, source_target_pairs={{0,2},{1,3},{2,0},{3,1},{4,6},{5,7},{6,4},{7,5},{8,10},{9,11},{10,... | collective-permute-start | bytes 1572872 | tf_op jit(solution)/shard_map/ppermute | solution.py:40
  109.3 37.4 %collective-permute-start.44 = (bf16[64,2048]{1,0:T(8,128)(2,1)S(1)}, bf16[64,2048]{1,0:T(8,128)(2,1)S(1)}, u32[]{:S(2)}, u32[]{:S(2)}) collective-permute-start(bf16[64,2048]{1,0:T(8,128)(2,1)S(1)} %add_convert_fusion.5), channel_id=1, source_target_pairs={{0,2},{1,3},{2,0},{3,1},{4,6},{5,7},{6,4},{7,5},{8,10},{9,11},{10,... | collective-permute-start | bytes 786440 | tf_op jit(solution)/shard_map/ppermute | solution.py:40
  111.0 10.8 %collective-permute-start.47 = (bf16[64,2048]{1,0:T(8,128)(2,1)S(1)}, bf16[64,2048]{1,0:T(8,128)(2,1)S(1)}, u32[]{:S(2)}, u32[]{:S(2)}) collective-permute-start(bf16[64,2048]{1,0:T(8,128)(2,1)S(1)} %slice.79), channel_id=1, source_target_pairs={{0,4},{1,5},{2,6},{3,7},{4,0},{5,1},{6,2},{7,3},{8,12},{9,13},{10,... | collective-permute-start | bytes 786440 | tf_op jit(solution)/shard_map/ppermute | solution.py:40
  111.4 27.2 %collective-permute-start.49 = (bf16[64,2048]{1,0:T(8,128)(2,1)S(1)}, bf16[64,2048]{1,0:T(8,128)(2,1)S(1)}, u32[]{:S(2)}, u32[]{:S(2)}) collective-permute-start(bf16[64,2048]{1,0:T(8,128)(2,1)S(1)} %slice.123), channel_id=1, source_target_pairs={{0,4},{1,5},{2,6},{3,7},{4,0},{5,1},{6,2},{7,3},{8,12},{9,13},{10,... | collective-permute-start | bytes 786440 | tf_op jit(solution)/shard_map/ppermute | solution.py:40
  121.4 16.9 %collective-permute-start.37 = (bf16[128,2048]{1,0:T(8,128)(2,1)S(1)}, bf16[128,2048]{1,0:T(8,128)(2,1)S(1)}, u32[]{:S(2)}, u32[]{:S(2)}) collective-permute-start(bf16[128,2048]{1,0:T(8,128)(2,1)S(1)} %add_convert_fusion.2), channel_id=1, source_target_pairs={{0,2},{1,3},{2,0},{3,1},{4,6},{5,7},{6,4},{7,5},{8,10},{9,11},{10,... | collective-permute-start | bytes 1572872 | tf_op jit(solution)/shard_map/ppermute | solution.py:40
  121.8 41.5 %collective-permute-start.40 = (bf16[64,2048]{1,0:T(8,128)(2,1)S(1)}, bf16[64,2048]{1,0:T(8,128)(2,1)S(1)}, u32[]{:S(2)}, u32[]{:S(2)}) collective-permute-start(bf16[64,2048]{1,0:T(8,128)(2,1)S(1)} %fusion.4), channel_id=1, source_target_pairs={{0,4},{1,5},{2,6},{3,7},{4,0},{5,1},{6,2},{7,3},{8,12},{9,13},{10,... | collective-permute-start | bytes 786440 | tf_op jit(solution)/shard_map/ppermute | solution.py:40
  144.1 17.9 %collective-permute-start.50 = (bf16[64,2048]{1,0:T(8,128)(2,1)S(1)}, bf16[64,2048]{1,0:T(8,128)(2,1)S(1)}, u32[]{:S(2)}, u32[]{:S(2)}) collective-permute-start(bf16[64,2048]{1,0:T(8,128)(2,1)S(1)} %fusion.1), channel_id=1, source_target_pairs={{0,8},{1,9},{2,10},{3,11},{4,12},{5,13},{6,14},{7,15},{8,0},{9,1},... | collective-permute-start | bytes 786440 | tf_op jit(solution)/shard_map/ppermute | solution.py:40
  145.5 22.2 %collective-permute-start.39 = (bf16[64,2048]{1,0:T(8,128)(2,1)S(1)}, bf16[64,2048]{1,0:T(8,128)(2,1)S(1)}, u32[]{:S(2)}, u32[]{:S(2)}) collective-permute-start(bf16[64,2048]{1,0:T(8,128)(2,1)S(1)} %fusion.7), channel_id=1, source_target_pairs={{0,8},{1,9},{2,10},{3,11},{4,12},{5,13},{6,14},{7,15},{8,0},{9,1},... | collective-permute-start | bytes 786440 | tf_op jit(solution)/shard_map/ppermute | solution.py:40
  (15 other events, 238.4 us)

commit v2 on v1

--- a/solution.py
+++ b/solution.py
@@ -27,6 +27,7 @@
 
 
 JOINED = (("b", 0), ("b", 1))
+PARTED = (("f", 0),)
 
 
 class Grid:
@@ -72,7 +73,12 @@
             if (name, g) in JOINED:
                 joined = self.swap(sent[block:], 4)
                 sent = (sent[:block].astype(f32) + joined.astype(f32)).astype(bf16)
+            if (name, g) in PARTED:
+                last = self.swap(sent[block:], 2)
+                sent = sent[:block]
             crossed = self.swap(sent, 2)
+            if (name, g) in PARTED:
+                crossed = jnp.concatenate([crossed, last], axis=0)
             for i, k in enumerate(group):
                 part = slice(i * block, (i + 1) * block)
                 total[k] = near[part]

time: 172 us -> 180 us (1.047)
  the two profiles are of different devices: /device:TPU:15 before, /device:TPU:0 now
where the time goes in v2:
time: 180 us
  waiting for transfers between devices  95.7 us (53%)
  starting transfers between devices  43.5 us (24%)
  Pallas kernels  31.6 us (18%)
  other arithmetic  5.98 us (3%)
  local copies, waits for them, and re-layouts  2.19 us (1%)
    ppermute x51, waiting for transfers between devices, swap(): return lax.ppermute(x, 'expert', [(i, i ^ bits) for i in range(self.size)])  90.1 us
    ppermute x51, starting transfers between devices, swap(): return lax.ppermute(x, 'expert', [(i, i ^ bits) for i in range(self.size)])  38.5 us
    pallas_call x2, Pallas kernels, expert_backward(): pl.pallas_call(lambda *refs: backward_kernel(experts, blocks, *refs), out...  15.8 us
    pallas_call x2, Pallas kernels, expert_forward(): pl.pallas_call(lambda *refs: forward_kernel(experts, len(rows), *refs), g...  12.3 us
    ppermute x1, waiting for transfers between devices, from_behind(): return lax.ppermute(block, axis, route)  5.59 us
  transfers between devices with their start and end apart: 53, of which 16 were waited for; matrix products, arithmetic and copies ran while one was open for 3% of the time, Pallas kernels for 18%

profile of v2, /device:TPU:0, one launch (start us, length us, event | category | flops | bytes accessed | tf_op | source)
XLA Modules:
  0.0 180.0 jit_solution(15202830664802310657)
XLA Ops:
  0.6 3.1 %collective-permute-start.8 = (bf16[64,2048]{1,0:T(8,128)(2,1)}, bf16[64,2048]{1,0:T(8,128)(2,1)S(1)}, u32[]{:S(2)}, u32[]{:S(2)}) collective-permute-start(bf16[64,2048]{1,0:T(8,128)(2,1)} %bitcast.40), channel_id=1, source_target_pairs={{0,16},{16,0},{1,17},{17,1},{2,18},{18,2},{3,19},{19,3},{4,20},{20... | collective-permute-start | bytes 786440 | tf_op jit(solution)/shard_map/ppermute | solution.py:22
  3.7 0.8 select_reduce_fusion.2
  4.4 1.1 fusion.12
  5.6 1.9 %collective-permute-start = (bf16[64,2048]{1,0:T(8,128)(2,1)S(1)}, bf16[64,2048]{1,0:T(8,128)(2,1)S(1)}, u32[]{:S(2)}, u32[]{:S(2)}) collective-permute-start(bf16[64,2048]{1,0:T(8,128)(2,1)S(1)} %fusion.12), channel_id=1, source_target_pairs={{0,16},{1,17},{2,18},{3,19},{4,20},{5,21},{6,22},{7,23},{8,24},{9,... | collective-permute-start | bytes 786440 | tf_op jit(solution)/shard_map/ppermute | solution.py:17
  7.5 0.7 select_reduce_fusion.1
  8.4 0.7 select_reduce_fusion
  9.5 5.6 %collective-permute-done.received = bf16[64,2048]{1,0:T(8,128)(2,1)S(1)} collective-permute-done((bf16[64,2048]{1,0:T(8,128)(2,1)S(1)}, bf16[64,2048]{1,0:T(8,128)(2,1)S(1)}, u32[]{:S(2)}, u32[]{:S(2)}) %collective-permute-start) | collective-permute-done | bytes 262176 | tf_op jit(solution)/shard_map/ppermute | solution.py:17
  15.1 0.9 copy-done.1
  16.7 0.9 normed_rows.1.refs_1_
  17.6 2.6 %collective-permute-start.19 = (bf16[64,2048]{1,0:T(8,128)(2,1)}, bf16[64,2048]{1,0:T(8,128)(2,1)}, u32[]{:S(2)}, u32[]{:S(2)}) collective-permute-start(bf16[64,2048]{1,0:T(8,128)(2,1)} %normed_rows.1.refs_1_), channel_id=1, source_target_pairs={{0,8},{1,9},{2,10},{3,11},{4,12},{5,13},{6,14},{7,15},{8,0},{9,1},... | collective-permute-start | bytes 786440 | tf_op jit(solution)/shard_map/ppermute | solution.py:41
  20.2 1.6 collective-permute-start.9
  21.9 1.5 collective-permute-start.10
  24.4 7.4 %collective-permute-done.19.refs_1_ = bf16[64,2048]{1,0:T(8,128)(2,1)} collective-permute-done((bf16[64,2048]{1,0:T(8,128)(2,1)}, bf16[64,2048]{1,0:T(8,128)(2,1)}, u32[]{:S(2)}, u32[]{:S(2)}) %collective-permute-start.19) | collective-permute-done | bytes 262176 | tf_op jit(solution)/shard_map/ppermute | solution.py:41
  31.8 6.0 %collective-permute-done.1.refs_2_ = bf16[64,2048]{1,0:T(8,128)(2,1)} collective-permute-done((bf16[64,2048]{1,0:T(8,128)(2,1)}, bf16[64,2048]{1,0:T(8,128)(2,1)}, u32[]{:S(2)}, u32[]{:S(2)}) %collective-permute-start.1) | collective-permute-done | bytes 262176 | tf_op jit(solution)/shard_map/ppermute | solution.py:41
  37.8 1.4 collective-permute-start.27
  39.2 1.6 collective-permute-start.20
  40.8 1.5 collective-permute-start.21
  43.0 1.5 collective-permute-start.3
  44.5 9.3 %collective-permute-done.27.refs_9_.refs_1_ = bf16[64,2176]{1,0:T(8,128)(2,1)S(1)} collective-permute-done((bf16[64,2176]{1,0:T(8,128)(2,1)S(1)}, bf16[64,2176]{1,0:T(8,128)(2,1)S(1)}, u32[]{:S(2)}, u32[]{:S(2)}) %collective-permute-start.27) | collective-permute-done | bytes 278560 | tf_op jit(solution)/shard_map/ppermute | solution.py:41
  54.3 1.9 %collective-permute-done.11.refs_12_.refs_4_ = bf16[64,2176]{1,0:T(8,128)(2,1)S(1)} collective-permute-done((bf16[64,2176]{1,0:T(8,128)(2,1)S(1)}, bf16[64,2176]{1,0:T(8,128)(2,1)S(1)}, u32[]{:S(2)}, u32[]{:S(2)}) %collective-permute-start.11) | collective-permute-done | bytes 278560 | tf_op jit(solution)/shard_map/ppermute | solution.py:41
  56.2 1.5 prepare.1.refs_9_
  57.7 3.1 %collective-permute-done.3.refs_4_ = bf16[64,2048]{1,0:T(8,128)(2,1)S(1)} collective-permute-done((bf16[64,2048]{1,0:T(8,128)(2,1)}, bf16[64,2048]{1,0:T(8,128)(2,1)S(1)}, u32[]{:S(2)}, u32[]{:S(2)}) %collective-permute-start.3) | collective-permute-done | bytes 262176 | tf_op jit(solution)/shard_map/ppermute | solution.py:41
  61.3 1.5 collective-permute-start.29
  62.9 1.5 collective-permute-start.30
  64.4 8.0 %expert_backward.2 = (bf16[128,2048]{1,0:T(8,128)(2,1)S(1)}, bf16[128,2048]{1,0:T(8,128)(2,1)S(1)}, bf16[128,2048]{1,0:T(8,128)(2,1)S(1)}, bf16[128,2048]{1,0:T(8,128)(2,1)S(1)}) custom-call(s32[9]{0:T(128)S(1)} %broadcast_xor_fusion.1.refs_0_, bf16[64,2176]{1,0:T(8,128)(2,1)S(1)} %pad_maximum_fusion.refs_9_.refs_1_, ...), custom_call_target="tpu_custom_call" | custom-call | flops 4831838208 | bytes 12582912 | tf_op jit(solution)/shard_map/expert_backward/pallas_call | solution.py:220
  73.8 2.4 %collective-permute-done.30.refs_12_.refs_4_ = bf16[64,2176]{1,0:T(8,128)(2,1)S(1)} collective-permute-done((bf16[64,2176]{1,0:T(8,128)(2,1)S(1)}, bf16[64,2176]{1,0:T(8,128)(2,1)S(1)}, u32[]{:S(2)}, u32[]{:S(2)}) %collective-permute-start.30) | collective-permute-done | bytes 278560 | tf_op jit(solution)/shard_map/ppermute | solution.py:41
  76.2 6.3 %expert_forward.2 = (bf16[128,2048]{1,0:T(8,128)(2,1)S(1)}, bf16[128,2048]{1,0:T(8,128)(2,1)S(1)}, bf16[128,2048]{1,0:T(8,128)(2,1)S(1)}, bf16[128,2048]{1,0:T(8,128)(2,1)S(1)}) custom-call(s32[9]{0:T(128)S(1)} %broadcast_xor_fusion.1.refs_0_, bf16[64,2048]{1,0:T(8,128)(2,1)} %normed_rows.1.refs_1_, bf16[64,2048]{1,0:T(8,128)(2,1)} %collective-permute-done.1.refs_2_, ...), custom_call_target="tpu_custom_call" | custom-call | flops 4831838208 | bytes 10485760 | tf_op jit(solution)/shard_map/expert_forward/pallas_call | solution.py:202
  84.1 7.7 %expert_backward.3 = (bf16[128,2048]{1,0:T(8,128)(2,1)S(1)}, bf16[128,2048]{1,0:T(8,128)(2,1)S(1)}, bf16[128,2048]{1,0:T(8,128)(2,1)S(1)}, bf16[128,2048]{1,0:T(8,128)(2,1)S(1)}) custom-call(s32[9]{0:T(128)S(1)} %broadcast_xor_fusion.refs_0_, bf16[64,2176]{1,0:T(8,128)(2,1)S(1)} %collective-permute-done.27.refs_9_.refs_1_, ...), custom_call_target="tpu_custom_call" | custom-call | flops 4831838208 | bytes 12582912 | tf_op jit(solution)/shard_map/expert_backward/pallas_call | solution.py:220
  93.0 6.0 %expert_forward.3 = (bf16[128,2048]{1,0:T(8,128)(2,1)S(1)}, bf16[128,2048]{1,0:T(8,128)(2,1)S(1)}, bf16[128,2048]{1,0:T(8,128)(2,1)S(1)}, bf16[128,2048]{1,0:T(8,128)(2,1)S(1)}) custom-call(s32[9]{0:T(128)S(1)} %broadcast_xor_fusion.refs_0_, bf16[64,2048]{1,0:T(8,128)(2,1)} %collective-permute-done.19.refs_1_, ...), custom_call_target="tpu_custom_call" | custom-call | flops 4831838208 | bytes 10485760 | tf_op jit(solution)/shard_map/expert_forward/pallas_call | solution.py:202
  100.4 2.2 %collective-permute-start.40 = (bf16[64,2048]{1,0:T(8,128)(2,1)S(1)}, bf16[64,2048]{1,0:T(8,128)(2,1)S(1)}, u32[]{:S(2)}, u32[]{:S(2)}) collective-permute-start(bf16[64,2048]{1,0:T(8,128)(2,1)S(1)} %get-tuple-element.35), channel_id=1, source_target_pairs={{0,2},{1,3},{2,0},{3,1},{4,6},{5,7},{6,4},{7,5},{8,10},{9,11},{10,... | collective-permute-start | bytes 786440 | tf_op jit(solution)/shard_map/ppermute | solution.py:41
  102.7 6.8 %collective-permute-done.40 = bf16[64,2048]{1,0:T(8,128)(2,1)S(1)} collective-permute-done((bf16[64,2048]{1,0:T(8,128)(2,1)S(1)}, bf16[64,2048]{1,0:T(8,128)(2,1)S(1)}, u32[]{:S(2)}, u32[]{:S(2)}) %collective-permute-start.40) | collective-permute-done | bytes 262176 | tf_op jit(solution)/shard_map/ppermute | solution.py:41
  110.0 7.6 %collective-permute-done.44 = bf16[64,2048]{1,0:T(8,128)(2,1)S(1)} collective-permute-done((bf16[64,2048]{1,0:T(8,128)(2,1)S(1)}, bf16[64,2048]{1,0:T(8,128)(2,1)S(1)}, u32[]{:S(2)}, u32[]{:S(2)}) %collective-permute-start.44) | collective-permute-done | bytes 262176 | tf_op jit(solution)/shard_map/ppermute | solution.py:41
  118.0 1.6 collective-permute-start.18
  120.4 1.7 collective-permute-start.48
  122.3 1.5 collective-permute-start.37
  124.0 6.3 %collective-permute-done.48 = bf16[64,2048]{1,0:T(8,128)(2,1)S(1)} collective-permute-done((bf16[64,2048]{1,0:T(8,128)(2,1)S(1)}, bf16[64,2048]{1,0:T(8,128)(2,1)S(1)}, u32[]{:S(2)}, u32[]{:S(2)}) %collective-permute-start.48) | collective-permute-done | bytes 262176 | tf_op jit(solution)/shard_map/ppermute | solution.py:41
  130.7 11.0 %collective-permute-done.37 = bf16[128,2048]{1,0:T(8,128)(2,1)S(1)} collective-permute-done((bf16[128,2048]{1,0:T(8,128)(2,1)S(1)}, bf16[128,2048]{1,0:T(8,128)(2,1)S(1)}, u32[]{:S(2)}, u32[]{:S(2)}) %collective-permute-start.37) | collective-permute-done | bytes 524320 | tf_op jit(solution)/shard_map/ppermute | solution.py:41
  141.7 1.3 collective-permute-start.49
  143.1 1.6 collective-permute-start.41
  144.8 3.3 %collective-permute-done.49 = bf16[64,2048]{1,0:T(8,128)(2,1)S(1)} collective-permute-done((bf16[64,2048]{1,0:T(8,128)(2,1)S(1)}, bf16[64,2048]{1,0:T(8,128)(2,1)S(1)}, u32[]{:S(2)}, u32[]{:S(2)}) %collective-permute-start.49) | collective-permute-done | bytes 262176 | tf_op jit(solution)/shard_map/ppermute | solution.py:41
  148.1 1.7 collective-permute-start.38
  149.9 5.3 %collective-permute-done.38 = bf16[64,2048]{1,0:T(8,128)(2,1)S(1)} collective-permute-done((bf16[64,2048]{1,0:T(8,128)(2,1)S(1)}, bf16[64,2048]{1,0:T(8,128)(2,1)S(1)}, u32[]{:S(2)}, u32[]{:S(2)}) %collective-permute-start.38) | collective-permute-done | bytes 262176 | tf_op jit(solution)/shard_map/ppermute | solution.py:41
  155.2 1.6 collective-permute-start.51
  156.9 1.4 collective-permute-start.39
  158.3 16.2 %collective-permute-done.51 = bf16[64,2048]{1,0:T(8,128)(2,1)S(1)} collective-permute-done((bf16[64,2048]{1,0:T(8,128)(2,1)S(1)}, bf16[64,2048]{1,0:T(8,128)(2,1)S(1)}, u32[]{:S(2)}, u32[]{:S(2)}) %collective-permute-start.51) | collective-permute-done | bytes 262176 | tf_op jit(solution)/shard_map/ppermute | solution.py:41
  174.7 1.1 gradient_rows.1
  175.7 3.3 %collective-permute-done.39 = bf16[64,2048]{1,0:T(8,128)(2,1)S(1)} collective-permute-done((bf16[64,2048]{1,0:T(8,128)(2,1)S(1)}, bf16[64,2048]{1,0:T(8,128)(2,1)S(1)}, u32[]{:S(2)}, u32[]{:S(2)}) %collective-permute-start.39) | collective-permute-done | bytes 262176 | tf_op jit(solution)/shard_map/ppermute | solution.py:41
  179.1 0.9 fusion.13
  (124 shorter events, 12.2 us)
Async XLA Ops:
  0.6 19.6 %collective-permute-start.8 = (bf16[64,2048]{1,0:T(8,128)(2,1)}, bf16[64,2048]{1,0:T(8,128)(2,1)S(1)}, u32[]{:S(2)}, u32[]{:S(2)}) collective-permute-start(bf16[64,2048]{1,0:T(8,128)(2,1)} %bitcast.40), channel_id=1, source_target_pairs={{0,16},{16,0},{1,17},{17,1},{2,18},{18,2},{3,19},{19,3},{4,20},{20... | collective-permute-start | bytes 786440 | tf_op jit(solution)/shard_map/ppermute | solution.py:22
  5.6 9.5 %collective-permute-start = (bf16[64,2048]{1,0:T(8,128)(2,1)S(1)}, bf16[64,2048]{1,0:T(8,128)(2,1)S(1)}, u32[]{:S(2)}, u32[]{:S(2)}) collective-permute-start(bf16[64,2048]{1,0:T(8,128)(2,1)S(1)} %fusion.12), channel_id=1, source_target_pairs={{0,16},{1,17},{2,18},{3,19},{4,20},{5,21},{6,22},{7,23},{8,24},{9,... | collective-permute-start | bytes 786440 | tf_op jit(solution)/shard_map/ppermute | solution.py:17
  17.6 14.1 %collective-permute-start.19 = (bf16[64,2048]{1,0:T(8,128)(2,1)}, bf16[64,2048]{1,0:T(8,128)(2,1)}, u32[]{:S(2)}, u32[]{:S(2)}) collective-permute-start(bf16[64,2048]{1,0:T(8,128)(2,1)} %normed_rows.1.refs_1_), channel_id=1, source_target_pairs={{0,8},{1,9},{2,10},{3,11},{4,12},{5,13},{6,14},{7,15},{8,0},{9,1},... | collective-permute-start | bytes 786440 | tf_op jit(solution)/shard_map/ppermute | solution.py:41
  20.2 20.6 %collective-permute-start.9 = (bf16[64,2176]{1,0:T(8,128)(2,1)S(1)}, bf16[64,2176]{1,0:T(8,128)(2,1)S(1)}, u32[]{:S(2)}, u32[]{:S(2)}) collective-permute-start(bf16[64,2176]{1,0:T(8,128)(2,1)S(1)} %pad_maximum_fusion.refs_9_.refs_1_), channel_id=1, source_target_pairs={{0,4},{1,5},{2,6},{3,7},{4,0},{5,1},{6,2},{7,3},{8,12},{9,13},{10,... | collective-permute-start | bytes 835592 | tf_op jit(solution)/shard_map/ppermute | solution.py:41
  21.9 20.4 %collective-permute-start.10 = (bf16[64,2176]{1,0:T(8,128)(2,1)S(1)}, bf16[64,2176]{1,0:T(8,128)(2,1)}, u32[]{:S(2)}, u32[]{:S(2)}) collective-permute-start(bf16[64,2176]{1,0:T(8,128)(2,1)S(1)} %pad_maximum_fusion.refs_9_.refs_1_), channel_id=1, source_target_pairs={{0,2},{1,3},{2,0},{3,1},{4,6},{5,7},{6,4},{7,5},{8,10},{9,11},{10,... | collective-permute-start | bytes 835592 | tf_op jit(solution)/shard_map/ppermute | solution.py:41
  23.4 14.4 %collective-permute-start.1 = (bf16[64,2048]{1,0:T(8,128)(2,1)}, bf16[64,2048]{1,0:T(8,128)(2,1)}, u32[]{:S(2)}, u32[]{:S(2)}) collective-permute-start(bf16[64,2048]{1,0:T(8,128)(2,1)} %normed_rows.1.refs_1_), channel_id=1, source_target_pairs={{0,4},{1,5},{2,6},{3,7},{4,0},{5,1},{6,2},{7,3},{8,12},{9,13},{10,... | collective-permute-start | bytes 786440 | tf_op jit(solution)/shard_map/ppermute | solution.py:41
  23.8 14.0 %collective-permute-start.2 = (bf16[64,2048]{1,0:T(8,128)(2,1)}, bf16[64,2048]{1,0:T(8,128)(2,1)}, u32[]{:S(2)}, u32[]{:S(2)}) collective-permute-start(bf16[64,2048]{1,0:T(8,128)(2,1)} %normed_rows.1.refs_1_), channel_id=1, source_target_pairs={{0,2},{1,3},{2,0},{3,1},{4,6},{5,7},{6,4},{7,5},{8,10},{9,11},{10,... | collective-permute-start | bytes 786440 | tf_op jit(solution)/shard_map/ppermute | solution.py:41
  31.8 7.5 %collective-permute-start.4 = (bf16[64,2048]{1,0:T(8,128)(2,1)}, bf16[64,2048]{1,0:T(8,128)(2,1)}, u32[]{:S(2)}, u32[]{:S(2)}) collective-permute-start(bf16[64,2048]{1,0:T(8,128)(2,1)} %normed_rows.1.refs_1_), channel_id=1, source_target_pairs={{0,1},{1,0},{2,3},{3,2},{4,5},{5,4},{6,7},{7,6},{8,9},{9,8},{10,11... | collective-permute-start | bytes 786440 | tf_op jit(solution)/shard_map/ppermute | solution.py:41
  37.8 15.9 %collective-permute-start.27 = (bf16[64,2176]{1,0:T(8,128)(2,1)S(1)}, bf16[64,2176]{1,0:T(8,128)(2,1)S(1)}, u32[]{:S(2)}, u32[]{:S(2)}) collective-permute-start(bf16[64,2176]{1,0:T(8,128)(2,1)S(1)} %pad_maximum_fusion.refs_9_.refs_1_), channel_id=1, source_target_pairs={{0,8},{1,9},{2,10},{3,11},{4,12},{5,13},{6,14},{7,15},{8,0},{9,1},... | collective-permute-start | bytes 835592 | tf_op jit(solution)/shard_map/ppermute | solution.py:41
  39.2 14.5 %collective-permute-start.20 = (bf16[64,2048]{1,0:T(8,128)(2,1)}, bf16[64,2048]{1,0:T(8,128)(2,1)S(1)}, u32[]{:S(2)}, u32[]{:S(2)}) collective-permute-start(bf16[64,2048]{1,0:T(8,128)(2,1)} %collective-permute-done.19.refs_1_), channel_id=1, source_target_pairs={{0,4},{1,5},{2,6},{3,7},{4,0},{5,1},{6,2},{7,3},{8,12},{9,13},{10,... | collective-permute-start | bytes 786440 | tf_op jit(solution)/shard_map/ppermute | solution.py:41
  40.8 13.4 %collective-permute-start.21 = (bf16[64,2048]{1,0:T(8,128)(2,1)}, bf16[64,2048]{1,0:T(8,128)(2,1)S(1)}, u32[]{:S(2)}, u32[]{:S(2)}) collective-permute-start(bf16[64,2048]{1,0:T(8,128)(2,1)} %collective-permute-done.19.refs_1_), channel_id=1, source_target_pairs={{0,2},{1,3},{2,0},{3,1},{4,6},{5,7},{6,4},{7,5},{8,10},{9,11},{10,... | collective-permute-start | bytes 786440 | tf_op jit(solution)/shard_map/ppermute | solution.py:41
  42.3 13.9 %collective-permute-start.11 = (bf16[64,2176]{1,0:T(8,128)(2,1)S(1)}, bf16[64,2176]{1,0:T(8,128)(2,1)S(1)}, u32[]{:S(2)}, u32[]{:S(2)}) collective-permute-start(bf16[64,2176]{1,0:T(8,128)(2,1)S(1)} %collective-permute-done.9.refs_10_.refs_2_), channel_id=1, source_target_pairs={{0,2},{1,3},{2,0},{3,1},{4,6},{5,7},{6,4},{7,5},{8,10},{9,11},{10,... | collective-permute-start | bytes 835592 | tf_op jit(solution)/shard_map/ppermute | solution.py:41
  43.0 17.8 %collective-permute-start.3 = (bf16[64,2048]{1,0:T(8,128)(2,1)}, bf16[64,2048]{1,0:T(8,128)(2,1)S(1)}, u32[]{:S(2)}, u32[]{:S(2)}) collective-permute-start(bf16[64,2048]{1,0:T(8,128)(2,1)} %collective-permute-done.1.refs_2_), channel_id=1, source_target_pairs={{0,2},{1,3},{2,0},{3,1},{4,6},{5,7},{6,4},{7,5},{8,10},{9,11},{10,... | collective-permute-start | bytes 786440 | tf_op jit(solution)/shard_map/ppermute | solution.py:41
  53.7 7.6 %collective-permute-start.14 = (bf16[64,2176]{1,0:T(8,128)(2,1)}, bf16[64,2176]{1,0:T(8,128)(2,1)S(1)}, u32[]{:S(2)}, u32[]{:S(2)}) collective-permute-start(bf16[64,2176]{1,0:T(8,128)(2,1)} %collective-permute-done.10.refs_11_.refs_3_), channel_id=1, source_target_pairs={{0,1},{1,0},{2,3},{3,2},{4,5},{5,4},{6,7},{7,6},{8,9},{9,8},{10,11... | collective-permute-start | bytes 835592 | tf_op jit(solution)/shard_map/ppermute | solution.py:41
  54.3 8.6 %collective-permute-start.28 = (bf16[64,2176]{1,0:T(8,128)(2,1)S(1)}, bf16[64,2176]{1,0:T(8,128)(2,1)S(1)}, u32[]{:S(2)}, u32[]{:S(2)}) collective-permute-start(bf16[64,2176]{1,0:T(8,128)(2,1)S(1)} %collective-permute-done.27.refs_9_.refs_1_), channel_id=1, source_target_pairs={{0,4},{1,5},{2,6},{3,7},{4,0},{5,1},{6,2},{7,3},{8,12},{9,13},{10,... | collective-permute-start | bytes 835592 | tf_op jit(solution)/shard_map/ppermute | solution.py:41
  60.8 11.6 %collective-permute-start.5 = (bf16[64,2048]{1,0:T(8,128)(2,1)}, bf16[64,2048]{1,0:T(8,128)(2,1)S(1)}, u32[]{:S(2)}, u32[]{:S(2)}) collective-permute-start(bf16[64,2048]{1,0:T(8,128)(2,1)} %collective-permute-done.1.refs_2_), channel_id=1, source_target_pairs={{0,1},{1,0},{2,3},{3,2},{4,5},{5,4},{6,7},{7,6},{8,9},{9,8},{10,11... | collective-permute-start | bytes 786440 | tf_op jit(solution)/shard_map/ppermute | solution.py:41
  60.8 11.9 %collective-permute-start.6 = (bf16[64,2048]{1,0:T(8,128)(2,1)}, bf16[64,2048]{1,0:T(8,128)(2,1)S(1)}, u32[]{:S(2)}, u32[]{:S(2)}) collective-permute-start(bf16[64,2048]{1,0:T(8,128)(2,1)} %collective-permute-done.2.refs_3_), channel_id=1, source_target_pairs={{0,1},{1,0},{2,3},{3,2},{4,5},{5,4},{6,7},{7,6},{8,9},{9,8},{10,11... | collective-permute-start | bytes 786440 | tf_op jit(solution)/shard_map/ppermute | solution.py:41
  61.3 12.0 %collective-permute-start.29 = (bf16[64,2176]{1,0:T(8,128)(2,1)S(1)}, bf16[64,2176]{1,0:T(8,128)(2,1)S(1)}, u32[]{:S(2)}, u32[]{:S(2)}) collective-permute-start(bf16[64,2176]{1,0:T(8,128)(2,1)S(1)} %collective-permute-done.27.refs_9_.refs_1_), channel_id=1, source_target_pairs={{0,2},{1,3},{2,0},{3,1},{4,6},{5,7},{6,4},{7,5},{8,10},{9,11},{10,... | collective-permute-start | bytes 835592 | tf_op jit(solution)/shard_map/ppermute | solution.py:41
  62.9 10.4 %collective-permute-start.7 = (bf16[64,2048]{1,0:T(8,128)(2,1)S(1)}, bf16[64,2048]{1,0:T(8,128)(2,1)S(1)}, u32[]{:S(2)}, u32[]{:S(2)}) collective-permute-start(bf16[64,2048]{1,0:T(8,128)(2,1)S(1)} %collective-permute-done.3.refs_4_), channel_id=1, source_target_pairs={{0,1},{1,0},{2,3},{3,2},{4,5},{5,4},{6,7},{7,6},{8,9},{9,8},{10,11... | collective-permute-start | bytes 786440 | tf_op jit(solution)/shard_map/ppermute | solution.py:41
  62.9 13.3 %collective-permute-start.30 = (bf16[64,2176]{1,0:T(8,128)(2,1)S(1)}, bf16[64,2176]{1,0:T(8,128)(2,1)S(1)}, u32[]{:S(2)}, u32[]{:S(2)}) collective-permute-start(bf16[64,2176]{1,0:T(8,128)(2,1)S(1)} %collective-permute-done.28.refs_10_.refs_2_), channel_id=1, source_target_pairs={{0,2},{1,3},{2,0},{3,1},{4,6},{5,7},{6,4},{7,5},{8,10},{9,11},{10,... | collective-permute-start | bytes 835592 | tf_op jit(solution)/shard_map/ppermute | solution.py:41
  72.4 10.1 %collective-permute-start.31 = (bf16[64,2176]{1,0:T(8,128)(2,1)S(1)}, bf16[64,2176]{1,0:T(8,128)(2,1)S(1)}, u32[]{:S(2)}, u32[]{:S(2)}) collective-permute-start(bf16[64,2176]{1,0:T(8,128)(2,1)S(1)} %collective-permute-done.27.refs_9_.refs_1_), channel_id=1, source_target_pairs={{0,1},{1,0},{2,3},{3,2},{4,5},{5,4},{6,7},{7,6},{8,9},{9,8},{10,11... | collective-permute-start | bytes 835592 | tf_op jit(solution)/shard_map/ppermute | solution.py:41
  72.7 10.4 %collective-permute-start.22 = (bf16[64,2048]{1,0:T(8,128)(2,1)S(1)}, bf16[64,2048]{1,0:T(8,128)(2,1)S(1)}, u32[]{:S(2)}, u32[]{:S(2)}) collective-permute-start(bf16[64,2048]{1,0:T(8,128)(2,1)S(1)} %collective-permute-done.20.refs_2_), channel_id=1, source_target_pairs={{0,2},{1,3},{2,0},{3,1},{4,6},{5,7},{6,4},{7,5},{8,10},{9,11},{10,... | collective-permute-start | bytes 786440 | tf_op jit(solution)/shard_map/ppermute | solution.py:41
  73.3 9.9 %collective-permute-start.32 = (bf16[64,2176]{1,0:T(8,128)(2,1)S(1)}, bf16[64,2176]{1,0:T(8,128)(2,1)S(1)}, u32[]{:S(2)}, u32[]{:S(2)}) collective-permute-start(bf16[64,2176]{1,0:T(8,128)(2,1)S(1)} %collective-permute-done.28.refs_10_.refs_2_), channel_id=1, source_target_pairs={{0,1},{1,0},{2,3},{3,2},{4,5},{5,4},{6,7},{7,6},{8,9},{9,8},{10,11... | collective-permute-start | bytes 835592 | tf_op jit(solution)/shard_map/ppermute | solution.py:41
  73.3 10.3 %collective-permute-start.33 = (bf16[64,2176]{1,0:T(8,128)(2,1)S(1)}, bf16[64,2176]{1,0:T(8,128)(2,1)S(1)}, u32[]{:S(2)}, u32[]{:S(2)}) collective-permute-start(bf16[64,2176]{1,0:T(8,128)(2,1)S(1)} %collective-permute-done.29.refs_11_.refs_3_), channel_id=1, source_target_pairs={{0,1},{1,0},{2,3},{3,2},{4,5},{5,4},{6,7},{7,6},{8,9},{9,8},{10,11... | collective-permute-start | bytes 835592 | tf_op jit(solution)/shard_map/ppermute | solution.py:41
  76.2 7.5 %collective-permute-start.34 = (bf16[64,2176]{1,0:T(8,128)(2,1)S(1)}, bf16[64,2176]{1,0:T(8,128)(2,1)S(1)}, u32[]{:S(2)}, u32[]{:S(2)}) collective-permute-start(bf16[64,2176]{1,0:T(8,128)(2,1)S(1)} %collective-permute-done.30.refs_12_.refs_4_), channel_id=1, source_target_pairs={{0,1},{1,0},{2,3},{3,2},{4,5},{5,4},{6,7},{7,6},{8,9},{9,8},{10,11... | collective-permute-start | bytes 835592 | tf_op jit(solution)/shard_map/ppermute | solution.py:41
  82.5 9.4 %collective-permute-start.23 = (bf16[64,2048]{1,0:T(8,128)(2,1)}, bf16[64,2048]{1,0:T(8,128)(2,1)S(1)}, u32[]{:S(2)}, u32[]{:S(2)}) collective-permute-start(bf16[64,2048]{1,0:T(8,128)(2,1)} %collective-permute-done.19.refs_1_), channel_id=1, source_target_pairs={{0,1},{1,0},{2,3},{3,2},{4,5},{5,4},{6,7},{7,6},{8,9},{9,8},{10,11... | collective-permute-start | bytes 786440 | tf_op jit(solution)/shard_map/ppermute | solution.py:41
  83.1 9.0 %collective-permute-start.24 = (bf16[64,2048]{1,0:T(8,128)(2,1)S(1)}, bf16[64,2048]{1,0:T(8,128)(2,1)S(1)}, u32[]{:S(2)}, u32[]{:S(2)}) collective-permute-start(bf16[64,2048]{1,0:T(8,128)(2,1)S(1)} %collective-permute-done.20.refs_2_), channel_id=1, source_target_pairs={{0,1},{1,0},{2,3},{3,2},{4,5},{5,4},{6,7},{7,6},{8,9},{9,8},{10,11... | collective-permute-start | bytes 786440 | tf_op jit(solution)/shard_map/ppermute | solution.py:41
  83.2 9.3 %collective-permute-start.25 = (bf16[64,2048]{1,0:T(8,128)(2,1)S(1)}, bf16[64,2048]{1,0:T(8,128)(2,1)S(1)}, u32[]{:S(2)}, u32[]{:S(2)}) collective-permute-start(bf16[64,2048]{1,0:T(8,128)(2,1)S(1)} %collective-permute-done.21.refs_3_), channel_id=1, source_target_pairs={{0,1},{1,0},{2,3},{3,2},{4,5},{5,4},{6,7},{7,6},{8,9},{9,8},{10,11... | collective-permute-start | bytes 786440 | tf_op jit(solution)/shard_map/ppermute | solution.py:41
  83.6 9.0 %collective-permute-start.26 = (bf16[64,2048]{1,0:T(8,128)(2,1)S(1)}, bf16[64,2048]{1,0:T(8,128)(2,1)S(1)}, u32[]{:S(2)}, u32[]{:S(2)}) collective-permute-start(bf16[64,2048]{1,0:T(8,128)(2,1)S(1)} %collective-permute-done.22.refs_4_), channel_id=1, source_target_pairs={{0,1},{1,0},{2,3},{3,2},{4,5},{5,4},{6,7},{7,6},{8,9},{9,8},{10,11... | collective-permute-start | bytes 786440 | tf_op jit(solution)/shard_map/ppermute | solution.py:41
  83.7 15.3 %collective-permute-start.43 = (bf16[128,2048]{1,0:T(8,128)(2,1)S(1)}, bf16[128,2048]{1,0:T(8,128)(2,1)S(1)}, u32[]{:S(2)}, u32[]{:S(2)}) collective-permute-start(bf16[128,2048]{1,0:T(8,128)(2,1)S(1)} %get-tuple-element.29), channel_id=1, source_target_pairs={{0,1},{1,0},{2,3},{3,2},{4,5},{5,4},{6,7},{7,6},{8,9},{9,8},{10,11... | collective-permute-start | bytes 1572872 | tf_op jit(solution)/shard_map/ppermute | solution.py:41
  91.9 7.5 %collective-permute-start.42 = (bf16[128,2048]{1,0:T(8,128)(2,1)S(1)}, bf16[128,2048]{1,0:T(8,128)(2,1)S(1)}, u32[]{:S(2)}, u32[]{:S(2)}) collective-permute-start(bf16[128,2048]{1,0:T(8,128)(2,1)S(1)} %get-tuple-element.27), channel_id=1, source_target_pairs={{0,1},{1,0},{2,3},{3,2},{4,5},{5,4},{6,7},{7,6},{8,9},{9,8},{10,11... | collective-permute-start | bytes 1572872 | tf_op jit(solution)/shard_map/ppermute | solution.py:41
  92.1 7.9 %collective-permute-start.17 = (bf16[128,2048]{1,0:T(8,128)(2,1)S(1)}, bf16[128,2048]{1,0:T(8,128)(2,1)S(1)}, u32[]{:S(2)}, u32[]{:S(2)}) collective-permute-start(bf16[128,2048]{1,0:T(8,128)(2,1)S(1)} %get-tuple-element.21), channel_id=1, source_target_pairs={{0,1},{1,0},{2,3},{3,2},{4,5},{5,4},{6,7},{7,6},{8,9},{9,8},{10,11... | collective-permute-start | bytes 1572872 | tf_op jit(solution)/shard_map/ppermute | solution.py:41
  92.5 7.9 %collective-permute-start.16 = (bf16[128,2048]{1,0:T(8,128)(2,1)S(1)}, bf16[128,2048]{1,0:T(8,128)(2,1)S(1)}, u32[]{:S(2)}, u32[]{:S(2)}) collective-permute-start(bf16[128,2048]{1,0:T(8,128)(2,1)S(1)} %get-tuple-element.19), channel_id=1, source_target_pairs={{0,1},{1,0},{2,3},{3,2},{4,5},{5,4},{6,7},{7,6},{8,9},{9,8},{10,11... | collective-permute-start | bytes 1572872 | tf_op jit(solution)/shard_map/ppermute | solution.py:41
  92.6 25.4 %collective-permute-start.47 = (bf16[128,2048]{1,0:T(8,128)(2,1)S(1)}, bf16[128,2048]{1,0:T(8,128)(2,1)S(1)}, u32[]{:S(2)}, u32[]{:S(2)}) collective-permute-start(bf16[128,2048]{1,0:T(8,128)(2,1)S(1)} %get-tuple-element.33), channel_id=1, source_target_pairs={{0,1},{1,0},{2,3},{3,2},{4,5},{5,4},{6,7},{7,6},{8,9},{9,8},{10,11... | collective-permute-start | bytes 1572872 | tf_op jit(solution)/shard_map/ppermute | solution.py:41
  99.1 21.3 %collective-permute-start.46 = (bf16[128,2048]{1,0:T(8,128)(2,1)S(1)}, bf16[128,2048]{1,0:T(8,128)(2,1)S(1)}, u32[]{:S(2)}, u32[]{:S(2)}) collective-permute-start(bf16[128,2048]{1,0:T(8,128)(2,1)S(1)} %get-tuple-element.31), channel_id=1, source_target_pairs={{0,1},{1,0},{2,3},{3,2},{4,5},{5,4},{6,7},{7,6},{8,9},{9,8},{10,11... | collective-permute-start | bytes 1572872 | tf_op jit(solution)/shard_map/ppermute | solution.py:41
  99.4 20.3 %collective-permute-start.36 = (bf16[128,2048]{1,0:T(8,128)(2,1)S(1)}, bf16[128,2048]{1,0:T(8,128)(2,1)S(1)}, u32[]{:S(2)}, u32[]{:S(2)}) collective-permute-start(bf16[128,2048]{1,0:T(8,128)(2,1)S(1)} %get-tuple-element.25), channel_id=1, source_target_pairs={{0,1},{1,0},{2,3},{3,2},{4,5},{5,4},{6,7},{7,6},{8,9},{9,8},{10,11... | collective-permute-start | bytes 1572872 | tf_op jit(solution)/shard_map/ppermute | solution.py:41
  100.0 22.3 %collective-permute-start.35 = (bf16[128,2048]{1,0:T(8,128)(2,1)S(1)}, bf16[128,2048]{1,0:T(8,128)(2,1)S(1)}, u32[]{:S(2)}, u32[]{:S(2)}) collective-permute-start(bf16[128,2048]{1,0:T(8,128)(2,1)S(1)} %get-tuple-element.23), channel_id=1, source_target_pairs={{0,1},{1,0},{2,3},{3,2},{4,5},{5,4},{6,7},{7,6},{8,9},{9,8},{10,11... | collective-permute-start | bytes 1572872 | tf_op jit(solution)/shard_map/ppermute | solution.py:41
  100.4 9.1 %collective-permute-start.40 = (bf16[64,2048]{1,0:T(8,128)(2,1)S(1)}, bf16[64,2048]{1,0:T(8,128)(2,1)S(1)}, u32[]{:S(2)}, u32[]{:S(2)}) collective-permute-start(bf16[64,2048]{1,0:T(8,128)(2,1)S(1)} %get-tuple-element.35), channel_id=1, source_target_pairs={{0,2},{1,3},{2,0},{3,1},{4,6},{5,7},{6,4},{7,5},{8,10},{9,11},{10,... | collective-permute-start | bytes 786440 | tf_op jit(solution)/shard_map/ppermute | solution.py:41
  109.5 8.1 %collective-permute-start.44 = (bf16[64,2048]{1,0:T(8,128)(2,1)S(1)}, bf16[64,2048]{1,0:T(8,128)(2,1)S(1)}, u32[]{:S(2)}, u32[]{:S(2)}) collective-permute-start(bf16[64,2048]{1,0:T(8,128)(2,1)S(1)} %slice.76), channel_id=1, source_target_pairs={{0,4},{1,5},{2,6},{3,7},{4,0},{5,1},{6,2},{7,3},{8,12},{9,13},{10,... | collective-permute-start | bytes 786440 | tf_op jit(solution)/shard_map/ppermute | solution.py:41
  117.5 39.3 %collective-permute-start.52 = (bf16[64,2048]{1,0:T(8,128)(2,1)S(1)}, bf16[64,2048]{1,0:T(8,128)(2,1)S(1)}, u32[]{:S(2)}, u32[]{:S(2)}) collective-permute-start(bf16[64,2048]{1,0:T(8,128)(2,1)S(1)} %slice.120), channel_id=1, source_target_pairs={{0,4},{1,5},{2,6},{3,7},{4,0},{5,1},{6,2},{7,3},{8,12},{9,13},{10,... | collective-permute-start | bytes 786440 | tf_op jit(solution)/shard_map/ppermute | solution.py:41
  118.0 57.8 %collective-permute-start.18 = (bf16[64,2048]{1,0:T(8,128)(2,1)S(1)}, bf16[64,2048]{1,0:T(8,128)(2,1)S(1)}, u32[]{:S(2)}, u32[]{:S(2)}) collective-permute-start(bf16[64,2048]{1,0:T(8,128)(2,1)S(1)} %get-tuple-element.34), channel_id=1, source_target_pairs={{0,2},{1,3},{2,0},{3,1},{4,6},{5,7},{6,4},{7,5},{8,10},{9,11},{10,... | collective-permute-start | bytes 786440 | tf_op jit(solution)/shard_map/ppermute | solution.py:41
  119.7 38.6 %collective-permute-start.45 = (bf16[64,2048]{1,0:T(8,128)(2,1)S(1)}, bf16[64,2048]{1,0:T(8,128)(2,1)S(1)}, u32[]{:S(2)}, u32[]{:S(2)}) collective-permute-start(bf16[64,2048]{1,0:T(8,128)(2,1)S(1)} %add_convert_fusion.5), channel_id=1, source_target_pairs={{0,2},{1,3},{2,0},{3,1},{4,6},{5,7},{6,4},{7,5},{8,10},{9,11},{10,... | collective-permute-start | bytes 786440 | tf_op jit(solution)/shard_map/ppermute | solution.py:41
  120.4 9.9 %collective-permute-start.48 = (bf16[64,2048]{1,0:T(8,128)(2,1)S(1)}, bf16[64,2048]{1,0:T(8,128)(2,1)S(1)}, u32[]{:S(2)}, u32[]{:S(2)}) collective-permute-start(bf16[64,2048]{1,0:T(8,128)(2,1)S(1)} %slice.79), channel_id=1, source_target_pairs={{0,4},{1,5},{2,6},{3,7},{4,0},{5,1},{6,2},{7,3},{8,12},{9,13},{10,... | collective-permute-start | bytes 786440 | tf_op jit(solution)/shard_map/ppermute | solution.py:41
  122.3 19.4 %collective-permute-start.37 = (bf16[128,2048]{1,0:T(8,128)(2,1)S(1)}, bf16[128,2048]{1,0:T(8,128)(2,1)S(1)}, u32[]{:S(2)}, u32[]{:S(2)}) collective-permute-start(bf16[128,2048]{1,0:T(8,128)(2,1)S(1)} %add_convert_fusion.2), channel_id=1, source_target_pairs={{0,2},{1,3},{2,0},{3,1},{4,6},{5,7},{6,4},{7,5},{8,10},{9,11},{10,... | collective-permute-start | bytes 1572872 | tf_op jit(solution)/shard_map/ppermute | solution.py:41
  130.3 12.8 %collective-permute-start.50 = (bf16[64,2048]{1,0:T(8,128)(2,1)S(1)}, bf16[64,2048]{1,0:T(8,128)(2,1)S(1)}, u32[]{:S(2)}, u32[]{:S(2)}) collective-permute-start(bf16[64,2048]{1,0:T(8,128)(2,1)S(1)} %slice.121), channel_id=1, source_target_pairs={{0,4},{1,5},{2,6},{3,7},{4,0},{5,1},{6,2},{7,3},{8,12},{9,13},{10,... | collective-permute-start | bytes 786440 | tf_op jit(solution)/shard_map/ppermute | solution.py:41
  143.1 32.6 %collective-permute-start.41 = (bf16[64,2048]{1,0:T(8,128)(2,1)S(1)}, bf16[64,2048]{1,0:T(8,128)(2,1)S(1)}, u32[]{:S(2)}, u32[]{:S(2)}) collective-permute-start(bf16[64,2048]{1,0:T(8,128)(2,1)S(1)} %fusion.4), channel_id=1, source_target_pairs={{0,4},{1,5},{2,6},{3,7},{4,0},{5,1},{6,2},{7,3},{8,12},{9,13},{10,... | collective-permute-start | bytes 786440 | tf_op jit(solution)/shard_map/ppermute | solution.py:41
  155.2 19.3 %collective-permute-start.51 = (bf16[64,2048]{1,0:T(8,128)(2,1)S(1)}, bf16[64,2048]{1,0:T(8,128)(2,1)S(1)}, u32[]{:S(2)}, u32[]{:S(2)}) collective-permute-start(bf16[64,2048]{1,0:T(8,128)(2,1)S(1)} %fusion.1), channel_id=1, source_target_pairs={{0,8},{1,9},{2,10},{3,11},{4,12},{5,13},{6,14},{7,15},{8,0},{9,1},... | collective-permute-start | bytes 786440 | tf_op jit(solution)/shard_map/ppermute | solution.py:41
  156.9 22.2 %collective-permute-start.39 = (bf16[64,2048]{1,0:T(8,128)(2,1)S(1)}, bf16[64,2048]{1,0:T(8,128)(2,1)S(1)}, u32[]{:S(2)}, u32[]{:S(2)}) collective-permute-start(bf16[64,2048]{1,0:T(8,128)(2,1)S(1)} %fusion.7), channel_id=1, source_target_pairs={{0,8},{1,9},{2,10},{3,11},{4,12},{5,13},{6,14},{7,15},{8,0},{9,1},... | collective-permute-start | bytes 786440 | tf_op jit(solution)/shard_map/ppermute | solution.py:41
  (16 other events, 276.5 us)
